TPU v7x, 32 devices: a whole 2x2x4 slice. The times are simulated.
32 devices in a mesh: scale: 2 (over y), lat: 16 (over z, x, core).
Axes of the slice: x: 2, y: 2, z: 4, core: 2. Of those that a mesh axis runs over, the one named last changes fastest.
Arguments:
- fine_state: float32 [16, 2, 1280, 1280], P(None, None, ('scale', 'lat')), may hold values from -6 to 6
- fine_noise: bfloat16 [16, 2, 1280, 1280], P(None, None, ('scale', 'lat')), may hold values from -6 to 6
- medium_state: float32 [16, 2, 640, 640], P(None, None, ('scale', 'lat')), may hold values from -6 to 6
- medium_noise: bfloat16 [16, 2, 640, 640], P(None, None, ('scale', 'lat')), may hold values from -6 to 6
- coarse_state: float32 [16, 2, 160, 160], P('lat'), may hold values from -6 to 6
- coarse_noise: bfloat16 [16, 2, 160, 160], P('lat'), may hold values from -6 to 6
- decay: float32 [3], replicated, may hold values from 0.5 to 0.95
- amplitude: float32 [3], replicated, may hold values from 0.3 to 1
- fine_basis: bfloat16 [1280, 32, 1280], P(('scale', 'lat')), may hold values from -0.0017089844 to 0.0017089844
- medium_basis: bfloat16 [640, 32, 640], P(('scale', 'lat')), may hold values from -0.0034179688 to 0.0034179688
- coarse_basis: bfloat16 [32, 160, 160], P(('scale', 'lat')), may hold values from -0.013671875 to 0.013671875
Outputs:
- fine_next: float32 [16, 2, 1280, 1280], P(None, None, ('scale', 'lat'))
- medium_next: float32 [16, 2, 640, 640], P(None, None, ('scale', 'lat'))
- coarse_next: float32 [16, 2, 160, 160], P('lat')
- pattern: float32 [16, 32, 2560], P(None, ('scale', 'lat'))
All inputs are finite; a program needn't handle non-finite values.
Results may differ from a plain program's by a relative error of at most 0.005.
Values may be sent and summed in bfloat16 or wider, within the bound.
A program may use at most 128 MiB of HBM per device.

v0:
```python
import functools
import math

import jax
import jax.numpy as jnp
import numpy as np
from jax import lax
from jax.experimental import pallas as pl
from jax.experimental.pallas import tpu as pltpu
from jax.sharding import PartitionSpec as P

NLON = 2560
LANES = 128
FOLD = NLON // LANES


def advance(state, noise, decay_rate, amp_rate, offset):
    slots = state.shape[3]
    mode_ids = offset + jnp.arange(state.shape[2], dtype=jnp.int32)
    degree_ids = jnp.arange(slots, dtype=jnp.int32)
    inside = mode_ids[:, None] + degree_ids[None, :] < slots
    updated = decay_rate * state + amp_rate * noise.astype(jnp.float32)
    return jnp.where(inside, updated, jnp.zeros_like(updated))


def phase_rows(block, devices):
    return max((p * block % FOLD + block - 1) // FOLD + 1 for p in range(devices))


def phase_blocks(fourier, place, devices, modes=None):
    rows, parts, block, members = fourier.shape
    high = phase_rows(block, devices)
    if block % FOLD:
        start = (place * block % FOLD).astype(jnp.int32)
        room = jnp.zeros((rows, parts, high * FOLD, members), fourier.dtype)
        zero = jnp.zeros((), jnp.int32)
        fourier = lax.dynamic_update_slice(room, fourier, (zero, zero, start, zero))
    return fourier.reshape(rows, parts * high, FOLD * members)


def received_rows(blocks, devices, width):
    source = np.arange(devices, dtype=np.int32)
    cols, parts = [], []
    for block in blocks:
        for part in range(2):
            for j in range(phase_rows(block, devices)):
                cols.append(source * block // FOLD + j)
                parts.append(part)
    while len(cols) < width:
        cols.append(source * 0)
        parts.append(0)
    high = np.stack(cols, axis=1).reshape(-1, 1)
    part = np.tile(np.array(parts, np.int32), devices)[:, None]
    return np.concatenate([high, part], axis=1).astype(np.int32)


def table_kernel(rows_ref, table_ref):
    count = rows_ref.shape[0]
    high, part = rows_ref[:, 0:1], rows_ref[:, 1:2]
    lon = lax.broadcasted_iota(jnp.int32, (count, LANES), 1)
    turns = (high * lon + part * (LANES // 4)) % LANES
    angle = turns.astype(jnp.float32) * (2.0 * math.pi / LANES)
    re, im = 2.0 * jnp.cos(angle), 2.0 * jnp.sin(angle)
    first = jnp.where(high == 0, 0.5, 1.0).astype(jnp.float32)
    shape = (-(-FOLD // 8) * 8, LANES)
    low = lax.broadcasted_iota(jnp.int32, shape, 0) * lax.broadcasted_iota(jnp.int32, shape, 1)
    low = low.astype(jnp.float32) * (2.0 * math.pi / NLON)
    cos, sin = jnp.cos(low), jnp.sin(low)
    for q in range(FOLD):
        cl, sl = cos[q : q + 1], sin[q : q + 1]
        real, imag = re * cl - im * sl, im * cl + re * sl
        if q == 0:
            real, imag = real * first, imag * first
        table_ref[q, :, :LANES] = real.astype(jnp.bfloat16)
        table_ref[q, :, LANES:] = imag.astype(jnp.bfloat16)


def longitude_kernel(members, got_ref, table_ref, out_ref):
    own = got_ref.shape[1]
    for i in range(own):
        spread = got_ref[:, i].astype(jnp.float32)
        spread = spread.reshape(spread.shape[0] * spread.shape[1], spread.shape[2])
        lanes = -spread.shape[1] % LANES
        if lanes:
            spread = jnp.concatenate(
                [spread, jnp.zeros((spread.shape[0], lanes), jnp.float32)], axis=1
            )
        turned = spread.T.astype(jnp.bfloat16)
        totals = [None] * FOLD
        for q in range(FOLD):
            part = jnp.dot(
                turned[q * members : (q + 1) * members],
                table_ref[q],
                preferred_element_type=jnp.float32,
            )
            real, imag = part[:, :LANES], part[:, LANES:]
            for h in range(FOLD):
                turn = 2.0 * math.pi * (q * h % FOLD) / FOLD
                term = math.cos(turn) * real - math.sin(turn) * imag
                totals[h] = term if q == 0 else totals[h] + term
        for h in range(FOLD):
            out_ref[:, i, h * LANES : (h + 1) * LANES] = jnp.tanh(totals[h])


def coarse_kernel(
    part_modes, decay_ref, amp_ref, state_ref, noise_ref, basis_ref, next_ref, mixed_ref, fine_ref, medium_ref
):
    held, parts, modes, slots = state_ref.shape
    for scale, rate_ref in ((0, fine_ref), (1, medium_ref)):
        rate_ref[0:1] = jnp.full((1, rate_ref.shape[1]), decay_ref[scale], jnp.float32)
        rate_ref[1:2] = jnp.full((1, rate_ref.shape[1]), amp_ref[scale], jnp.float32)
    mode_ids = lax.broadcasted_iota(jnp.int32, (modes, slots), 0)
    degree_ids = lax.broadcasted_iota(jnp.int32, (modes, slots), 1)
    inside = mode_ids + degree_ids < slots
    planes = []
    for e in range(held):
        for c in range(parts):
            new = decay_ref[2] * state_ref[e, c] + amp_ref[2] * noise_ref[e, c].astype(jnp.float32)
            new = jnp.where(inside, new, 0.0)
            next_ref[e, c] = new
            planes.append(new)
    for r in range(basis_ref.shape[0]):
        planes.append(basis_ref[r].astype(jnp.float32))
    empty = jnp.zeros((part_modes, slots), jnp.float32)
    for d in range(mixed_ref.shape[0]):
        pieces = []
        for plane in planes:
            piece = plane[d * part_modes : min((d + 1) * part_modes, modes)]
            missing = part_modes - piece.shape[0]
            if missing == part_modes:
                piece = empty
            elif missing:
                piece = jnp.concatenate([piece, empty[:missing]], axis=0)
            pieces.append(piece)
        mixed_ref[d] = jnp.concatenate(pieces, axis=0).astype(jnp.bfloat16)


def body(
    fine_state,
    fine_noise,
    medium_state,
    medium_noise,
    coarse_state,
    coarse_noise,
    decay,
    amplitude,
    fine_basis,
    medium_basis,
    coarse_basis,
):
    devices = lax.axis_size("scale") * lax.axis_size("lat")
    lat = lax.axis_size("lat")
    held, _, modes, slots = coarse_state.shape
    own = coarse_basis.shape[0]
    part_modes = -(-modes // devices)
    vmem = pl.BlockSpec(memory_space=pltpu.VMEM)
    smem = pl.BlockSpec(memory_space=pltpu.SMEM)
    coarse_next, mixed, fine_rates, medium_rates = pl.pallas_call(
        functools.partial(coarse_kernel, part_modes),
        out_shape=(
            jax.ShapeDtypeStruct(coarse_state.shape, jnp.float32),
            jax.ShapeDtypeStruct((devices, (2 * held + own) * part_modes, slots), jnp.bfloat16),
            jax.ShapeDtypeStruct((2, fine_state.shape[3]), jnp.float32),
            jax.ShapeDtypeStruct((2, medium_state.shape[3]), jnp.float32),
        ),
        in_specs=[smem, smem, vmem, vmem, vmem],
        out_specs=(vmem,) * 4,
    )(decay, amplitude, coarse_state, coarse_noise, coarse_basis)
    mixed = lax.all_to_all(mixed, ("scale", "lat"), split_axis=0, concat_axis=0, tiled=True)
    mixed = mixed.reshape(devices, 2 * held + own, part_modes, slots)
    coarse_half = mixed[:lat, : 2 * held].reshape(lat * held, 2, part_modes, slots)
    coarse_rows = mixed[:, 2 * held :].reshape(devices * own, part_modes, slots)
    place = lax.axis_index(("scale", "lat"))
    fine_next = advance(fine_state, fine_noise, fine_rates[0], fine_rates[1], place * fine_state.shape[2])
    medium_next = advance(
        medium_state, medium_noise, medium_rates[0], medium_rates[1], place * medium_state.shape[2]
    )
    fourier = []
    for half, basis, form in (
        (fine_next.astype(jnp.bfloat16), fine_basis, "ecmk,mrk->rcme"),
        (medium_next.astype(jnp.bfloat16), medium_basis, "ecmk,mrk->rcme"),
        (coarse_half, coarse_rows, "ecmk,rmk->rcme"),
    ):
        fourier.append(
            jnp.einsum(form, half, basis, preferred_element_type=jnp.float32).astype(jnp.bfloat16)
        )
    members = coarse_half.shape[0]
    blocks = [x.shape[2] for x in fourier]
    both = jnp.concatenate([phase_blocks(x, place, devices) for x in fourier], axis=1)
    width = -(-both.shape[1] // 8) * 8
    both = jnp.pad(both, ((0, 0), (0, width - both.shape[1]), (0, 0)))
    received = received_rows(blocks, devices, width)
    table = pl.pallas_call(
        table_kernel,
        out_shape=jax.ShapeDtypeStruct((FOLD, devices * width, 2 * LANES), jnp.bfloat16),
        in_specs=[vmem],
        out_specs=vmem,
        cost_estimate=pl.CostEstimate(
            flops=30 * FOLD * devices * width * LANES,
            bytes_accessed=8 * FOLD * devices * width * LANES,
            transcendentals=4 * devices * width * LANES,
        ),
    )(jnp.asarray(received))
    got = lax.all_to_all(both, ("scale", "lat"), split_axis=0, concat_axis=0, tiled=True)
    got = got.reshape(devices, own, width, FOLD * members)
    pattern = pl.pallas_call(
        functools.partial(longitude_kernel, members),
        out_shape=jax.ShapeDtypeStruct((members, own, NLON), jnp.float32),
        in_specs=[vmem, vmem],
        out_specs=vmem,
    )(got, table)
    return (fine_next, medium_next, coarse_next, pattern)


def solution(mesh):
    return jax.shard_map(
        body,
        mesh=mesh,
        in_specs=(
            P(None, None, ("scale", "lat"), None),
            P(None, None, ("scale", "lat"), None),
            P(None, None, ("scale", "lat"), None),
            P(None, None, ("scale", "lat"), None),
            P("lat", None, None, None),
            P("lat", None, None, None),
            P(),
            P(),
            P(("scale", "lat"), None, None),
            P(("scale", "lat"), None, None),
            P(("scale", "lat"), None, None),
        ),
        out_specs=(
            P(None, None, ("scale", "lat"), None),
            P(None, None, ("scale", "lat"), None),
            P("lat", None, None, None),
            P(None, ("scale", "lat"), None),
        ),
        check_vma=False,
    )
```

profile of v0, /device:TPU:0, one launch (start us, length us, event | category | flops | bytes accessed | tf_op | source)
XLA Modules:
  0.0 54.3 jit_solution(7914022533490892389)
XLA Ops:
  0.6 0.0 copy-start
  0.6 2.2 %shard_map.147 = (f32[1,2,160,160]{3,2,1,0:T(8,128)}, bf16[32,15,160]{2,1,0:T(8,128)(2,1)}, f32[2,1280]{1,0:T(2,128)}, f32[2,640]{1,0:T(2,128)}) custom-call(f32[3]{0:T(128)} %decay_ref.1, f32[3]{0:T(128)} %amp_ref.1, f32[1,2,160,160]{3,2,1,0:T(8,128)} %state_ref.1, bf16[1,2,160,160]{3,2,1,0:T(8,128)(2,1)} %noise_ref.1, bf16[1,160,160]{2,1,0:T(8,128)(2,1)} %basis_ref.1), custom_call_target="tpu_custom_call" | custom-call | tf_op jit(solution)/shard_map/pallas_call | solution.py:158
  2.8 7.3 %all-to-all-start = ((bf16[32,15,160]{2,1,0:T(8,128)(2,1)}), bf16[32,15,160]{2,1,0:T(8,128)(2,1)S(1)}, u32[]{:S(2)}, u32[]{:S(2)}) async-start(bf16[32,15,160]{2,1,0:T(8,128)(2,1)} %get-tuple-element.11), calls=%async_computation | async-start | bytes 524288 | tf_op jit(solution)/shard_map/all_to_all | solution.py:169
  10.1 0.8 %slice_reduce_fusion.1 = (f32[1280]{0:T(1024)S(1)}, f32[1280]{0:T(1024)S(1)}) fusion(f32[2,1280]{1,0:T(2,128)} %get-tuple-element.8), kind=kLoop, calls=%fused_computation.20 | loop fusion | bytes 20480 | tf_op jit(solution)/shard_map/slice | solution.py:174
  11.0 0.7 %add_compare_fusion = pred[40,1280]{1,0:T(8,128)(4,1)} fusion(s32[40]{0:T(128)S(1)} %iota_add_fusion.1), kind=kLoop, calls=%fused_computation.13 | loop fusion | flops 102400 | bytes 51360 | tf_op jit(solution)/shard_map/lt | solution.py:21
  11.7 1.4 %slice_reduce_fusion.3 = (f32[640]{0:T(1024)}, f32[640]{0:T(1024)}) fusion(f32[2,640]{1,0:T(2,128)} %get-tuple-element.9), kind=kLoop, calls=%fused_computation.22 | loop fusion | bytes 10240 | tf_op jit(solution)/shard_map/slice | solution.py:176
  13.1 0.1 add_compare_fusion.1
  13.2 7.9 %fusion.18 = (bf16[16,2,40,1280]{3,2,1,0:T(8,128)(2,1)S(1)}, f32[16,2,40,1280]{3,2,1,0:T(8,128)}) fusion(bf16[16,2,40,1280]{3,2,1,0:T(8,128)(2,1)} %param.13, f32[1280]{0:T(1024)S(1)} %get-tuple-element.13, f32[16,2,40,1280]{3,2,1,0:T(8,128)} %param.12, f32[1280]{0:T(1024)S(1)} %get-tuple-element.12, pred[40,1280]{1,0:T(8,128)(4,1)} %add_compare_fusion), kind=kLoop, calls=%fused_computation.25 | loop fusion | flops 9830400 | bytes 19722240 | tf_op jit(solution)/shard_map/convert_element_type | solution.py:180
  21.0 0.0 copy-done
  21.0 0.0 copy-start.1
  21.0 0.0 copy-start.5
  21.0 2.0 %fusion.8 = bf16[32,2,40,16]{0,3,1,2:T(8,128)(2,1)} fusion(bf16[40,32,1280]{2,1,0:T(8,128)(2,1)S(1)} %copy-done, bf16[16,2,40,1280]{3,2,1,0:T(8,128)(2,1)S(1)} %get-tuple-element.16), kind=kOutput, calls=%fused_computation.6 | convolution fusion | flops 104898560 | bytes 6635520 | tf_op jit(solution)/shard_map/ecmk,mrk->rcme/dot_general | solution.py:185
  23.1 0.0 copy-done.1
  23.1 0.0 copy-done.2
  23.1 0.0 copy-done.4
  23.1 0.0 copy-done.5
  23.1 2.8 %fusion.19 = (bf16[16,2,20,640]{3,1,2,0:T(2,128)(2,1)}, f32[16,2,20,640]{3,1,2,0:T(2,128)}) fusion(bf16[16,2,20,640]{3,1,2,0:T(2,128)(2,1)S(1)} %copy-done.2, f32[640]{0:T(1024)S(1)} %copy-done.5, f32[16,2,20,640]{3,1,2,0:T(2,128)S(1)} %copy-done.1, f32[640]{0:T(1024)S(1)} %copy-done.4, pred[20,640]{1,0:T(8,128)(4,1)S(1)} %add_compare_fusion.1), kind=kLoop, calls=%fused_computation.26 | loop fusion | flops 2457600 | bytes 4933120 | tf_op jit(solution)/shard_map/convert_element_type | solution.py:181
  25.9 1.7 %copy.24 = bf16[32,2,40,16]{0,3,2,1:T(8,128)(2,1)} copy(bf16[32,2,40,16]{0,3,1,2:T(8,128)(2,1)} %fusion.8) | data formatting | bytes 163840 | tf_op jit(solution)/shard_map/convert_element_type | solution.py:185
  27.6 1.8 %copy.30 = bf16[32,4,320]{2,1,0:T(4,128)(2,1)} copy(bf16[32,4,320]{0,2,1:T(8,128)(2,1)} %bitcast.31) | data formatting | bytes 163840 | tf_op jit(solution)/shard_map/reshape | solution.py:38
  29.4 1.8 %fusion.13 = bf16[32,2,20,16]{0,3,1,2:T(8,128)(2,1)S(1)} fusion(bf16[20,32,640]{2,1,0:T(8,128)(2,1)} %param.21, bf16[16,2,20,640]{3,1,2,0:T(2,128)(2,1)} %get-tuple-element.18), kind=kOutput, calls=%fused_computation.8 | convolution fusion | flops 26234880 | bytes 1679360 | tf_op jit(solution)/shard_map/ecmk,mrk->rcme/dot_general | solution.py:185
  31.2 0.7 %copy.26 = bf16[32,2,20,16]{0,3,2,1:T(8,128)(2,1)} copy(bf16[32,2,20,16]{0,3,1,2:T(8,128)(2,1)S(1)} %fusion.13) | data formatting | bytes 81920 | tf_op jit(solution)/shard_map/convert_element_type | solution.py:185
  31.9 1.7 %copy.31 = bf16[32,2,320]{2,1,0:T(2,128)(2,1)} copy(bf16[32,2,320]{0,2,1:T(8,128)(2,1)} %bitcast.34) | data formatting | bytes 81920 | tf_op jit(solution)/shard_map/reshape | solution.py:38
  33.5 0.0 all-to-all-done
  33.5 0.1 copy.27
  33.6 0.1 fusion.14
  33.8 0.1 copy.32
  33.9 1.8 %pad_maximum_fusion = bf16[32,8,320]{2,1,0:T(8,128)(2,1)} fusion(bf16[32,2,320]{2,1,0:T(2,128)(2,1)S(1)} %copy.32, bf16[32,2,320]{2,1,0:T(2,128)(2,1)} %copy.31, bf16[32,4,320]{2,1,0:T(4,128)(2,1)} %copy.30), kind=kLoop, calls=%fused_computation.14 | loop fusion | flops 491520 | bytes 327680 | tf_op jit(solution)/shard_map/concatenate | solution.py:189
  35.7 5.8 %all-to-all-start.1 = ((bf16[32,8,320]{2,1,0:T(8,128)(2,1)}), bf16[32,8,320]{2,1,0:T(8,128)(2,1)S(1)}, u32[]{:S(2)}, u32[]{:S(2)}) async-start(bf16[32,8,320]{2,1,0:T(8,128)(2,1)} %pad_maximum_fusion), calls=%async_computation.1 | async-start | bytes 393216 | tf_op jit(solution)/shard_map/all_to_all | solution.py:204
  41.6 4.2 %shard_map.148.table_ref = bf16[20,256,256]{2,1,0:T(8,128)(2,1)} custom-call(s32[256,2]{1,0:T(8,128)} %constant.37.clone.rows_ref), custom_call_target="tpu_custom_call" | custom-call | flops 19660800 | bytes 5242880 | tf_op jit(solution)/shard_map/pallas_call | solution.py:193
  45.7 4.8 %all-to-all-done.1 = bf16[32,8,320]{2,1,0:T(8,128)(2,1)S(1)} async-done(((bf16[32,8,320]{2,1,0:T(8,128)(2,1)}), bf16[32,8,320]{2,1,0:T(8,128)(2,1)S(1)}, u32[]{:S(2)}, u32[]{:S(2)}) %all-to-all-start.1) | async-done | bytes 163872 | tf_op jit(solution)/shard_map/all_to_all | solution.py:204
  50.5 0.7 %copy-done.3 = bf16[32,8,320]{2,1,0:T(8,128)(2,1)} copy-done((bf16[32,8,320]{2,1,0:T(8,128)(2,1)}, bf16[32,8,320]{2,1,0:T(8,128)(2,1)S(1)}, u32[]{:S(2)}) %copy-start.3) | copy-done | bytes 163864
  51.2 3.1 %shard_map.149 = f32[16,1,2560]{2,1,0:T(1,128)} custom-call(bf16[32,1,8,320]{3,2,1,0:T(8,128)(2,1)} %bitcast.32, bf16[20,256,256]{2,1,0:T(8,128)(2,1)} %shard_map.148.table_ref), custom_call_target="tpu_custom_call" | custom-call | tf_op jit(solution)/shard_map/pallas_call | solution.py:206
  (7 shorter events, 0.1 us)
Async XLA Ops:
  0.6 20.4 %copy-start = (bf16[40,32,1280]{2,1,0:T(8,128)(2,1)S(1)}, bf16[40,32,1280]{2,1,0:T(8,128)(2,1)}, u32[]{:S(2)}) copy-start(bf16[40,32,1280]{2,1,0:T(8,128)(2,1)} %param.20) | copy-start | bytes 9830404
  2.8 30.7 %all-to-all-start = ((bf16[32,15,160]{2,1,0:T(8,128)(2,1)}), bf16[32,15,160]{2,1,0:T(8,128)(2,1)S(1)}, u32[]{:S(2)}, u32[]{:S(2)}) async-start(bf16[32,15,160]{2,1,0:T(8,128)(2,1)} %get-tuple-element.11), calls=%async_computation | async-start | bytes 524288 | tf_op jit(solution)/shard_map/all_to_all | solution.py:169
  21.0 2.1 %copy-start.1 = (f32[16,2,20,640]{3,1,2,0:T(2,128)S(1)}, f32[16,2,20,640]{3,1,2,0:T(2,128)}, u32[]{:S(2)}) copy-start(f32[16,2,20,640]{3,1,2,0:T(2,128)} %param.14) | copy-start | bytes 4915204
  21.0 2.1 %copy-start.2 = (bf16[16,2,20,640]{3,1,2,0:T(2,128)(2,1)S(1)}, bf16[16,2,20,640]{3,1,2,0:T(2,128)(2,1)}, u32[]{:S(2)}) copy-start(bf16[16,2,20,640]{3,1,2,0:T(2,128)(2,1)} %param.15) | copy-start | bytes 2457604
  21.0 2.1 %copy-start.4 = (f32[640]{0:T(1024)S(1)}, f32[640]{0:T(1024)}, u32[]{:S(2)}) copy-start(f32[640]{0:T(1024)} %get-tuple-element.14) | copy-start | bytes 7684
  21.0 2.1 %copy-start.5 = (f32[640]{0:T(1024)S(1)}, f32[640]{0:T(1024)}, u32[]{:S(2)}) copy-start(f32[640]{0:T(1024)} %get-tuple-element.15) | copy-start | bytes 7684
  35.7 14.8 %all-to-all-start.1 = ((bf16[32,8,320]{2,1,0:T(8,128)(2,1)}), bf16[32,8,320]{2,1,0:T(8,128)(2,1)S(1)}, u32[]{:S(2)}, u32[]{:S(2)}) async-start(bf16[32,8,320]{2,1,0:T(8,128)(2,1)} %pad_maximum_fusion), calls=%async_computation.1 | async-start | bytes 393216 | tf_op jit(solution)/shard_map/all_to_all | solution.py:204
  50.5 0.7 %copy-start.3 = (bf16[32,8,320]{2,1,0:T(8,128)(2,1)}, bf16[32,8,320]{2,1,0:T(8,128)(2,1)S(1)}, u32[]{:S(2)}) copy-start(bf16[32,8,320]{2,1,0:T(8,128)(2,1)S(1)} %all-to-all-done.1) | copy-start | bytes 491524
where the time goes:
time: 54.9 us; the launch traced here: 54.3 us
  other arithmetic  13.3 us (24%)
  starting transfers between devices  13.2 us (24%)
  Pallas kernels  9.46 us (17%)
  local copies, waits for them, and re-layouts  8.99 us (16%)
  waiting for transfers between devices  4.78 us (9%)
  matrix products  3.94 us (7%)
  between operations  0.74 us (1%)
    convert_element_type x1, other arithmetic, body(): fine_next.astype(jnp.bfloat16)  7.86 us
    all_to_all x1, starting transfers between devices, body(): lax.all_to_all(mixed, ('scale', 'lat'), split_axis=0, concat_axis=0, tile...  7.33 us
    all_to_all x1, starting transfers between devices, body(): lax.all_to_all(both, ('scale', 'lat'), split_axis=0, concat_axis=0, tiled...  5.83 us
    all_to_all x1, waiting for transfers between devices, body(): lax.all_to_all(both, ('scale', 'lat'), split_axis=0, concat_axis=0, tiled...  4.78 us
    pallas_call x1, Pallas kernels, body(): pl.pallas_call(table_kernel, out_shape=jax.ShapeDtypeStruct((FOLD, device...  4.17 us
    dot_general x3, matrix products, body(): jnp.einsum(form, half, basis, preferred_element_type=jnp.float32)  3.94 us
    reshape x3, local copies, waits for them, and re-layouts, phase_blocks(): return fourier.reshape(rows, parts * high, FOLD * members)  3.55 us
    pallas_call x1, Pallas kernels, body(): pl.pallas_call(functools.partial(longitude_kernel, members), out_shape=ja...  3.14 us
  transfers between devices with their start and end apart: 2, of which 1 were waited for; matrix products, arithmetic and copies ran while one was open for 43% of the time, Pallas kernels for 8%

commit v1 on v0

--- a/solution.py
+++ b/solution.py
@@ -135,7 +135,7 @@
         mixed_ref[d] = jnp.concatenate(pieces, axis=0).astype(jnp.bfloat16)
 
 
-def body(
+def general_body(
     fine_state,
     fine_noise,
     medium_state,
@@ -212,6 +212,634 @@
     return (fine_next, medium_next, coarse_next, pattern)
 
 
+MESH = pl.DeviceIdType.MESH
+SUB = 8
+
+
+class Sizes:
+    def __init__(self, fine_state, medium_state, coarse_state, fine_basis, coarse_basis, scale, lat):
+        self.scale, self.lat, self.n = scale, lat, scale * lat
+        _, self.parts, self.fine, self.fine_slots = fine_state.shape
+        self.members = fine_state.shape[0]
+        self.pairs = self.members * self.parts
+        self.medium, self.medium_slots = medium_state.shape[2:]
+        self.coarse, self.coarse_slots = coarse_state.shape[2:]
+        self.held, self.own, self.rows = coarse_state.shape[0], coarse_basis.shape[0], fine_basis.shape[1]
+        self.groups = self.fine // SUB
+        self.quad = LANES // self.pairs
+        self.piece = self.coarse // lat
+        self.wrap = NLON // max(self.quad, 1)
+
+    def fits(self):
+        if self.pairs * 4 != LANES or self.parts != 2 or self.held != 1 or self.own != 1:
+            return False
+        if self.rows != self.n or self.members != self.lat or self.members != 16:
+            return False
+        if self.fine % SUB or self.medium % 4 or self.fine != 2 * self.medium:
+            return False
+        if self.fine_slots % LANES or self.medium_slots % LANES or self.coarse % self.lat:
+            return False
+        if self.piece != 2 * (self.medium // 4) or 3 * self.piece > 32 or self.piece + 2 > 12:
+            return False
+        if not LANES < self.coarse_slots <= 2 * LANES or self.coarse_slots != self.coarse:
+            return False
+        high = self.fine // 4
+        return SUB <= high and high - SUB + self.medium // 4 <= SUB and self.wrap % LANES == 0
+
+
+def turns(count, columns, period, index):
+    lon = lax.broadcasted_iota(jnp.int32, (count, columns), 1)
+    angle = ((index * lon) % period).astype(jnp.float32) * (2.0 * math.pi / period)
+    return jnp.cos(angle), jnp.sin(angle)
+
+
+def spread_kernel(
+    z,
+    decay,
+    amp,
+    fine_state,
+    fine_noise,
+    fine_basis,
+    medium_state,
+    medium_noise,
+    medium_basis,
+    coarse_state,
+    coarse_noise,
+    coarse_basis,
+    fine_next,
+    medium_next,
+    coarse_next,
+    got,
+    got_coarse,
+    table,
+    noise_f,
+    basis_f,
+    half,
+    picked,
+    noise_m,
+    basis_m,
+    half_m,
+    rows_f,
+    send,
+    noise_c,
+    basis_c,
+    first,
+    first_far,
+    landed,
+    landed_far,
+    landed_f,
+    left_c,
+    right_c,
+    rows_c,
+    second,
+    wave_cos,
+    wave_sin,
+    load_f,
+    load_m,
+    load_c,
+    sent,
+    came,
+    sent_one,
+    came_one,
+    sent_far,
+    came_far,
+    sent_two,
+    came_two,
+):
+    n, lat = z.n, z.lat
+    s, a = lax.axis_index("scale"), lax.axis_index("lat")
+    me = s * lat + a
+    f32, bf16 = jnp.float32, jnp.bfloat16
+    mid_tiles = z.medium_slots // LANES
+    fine_quads, medium_quads = z.fine // 4, z.medium // 4
+    far = -(-(z.coarse_slots - LANES) // z.piece)
+
+    def place(p):
+        return {"scale": p // lat, "lat": p % lat}
+
+    barrier = pltpu.get_barrier_semaphore()
+
+    def greet(i, _):
+        pl.semaphore_signal(barrier, inc=1, device_id=place((me + i) % n), device_id_type=MESH)
+        return 0
+
+    lax.fori_loop(1, n, greet, 0)
+
+    def coarse_loads():
+        return (
+            pltpu.make_async_copy(coarse_state.at[0], coarse_next, load_c.at[0]),
+            pltpu.make_async_copy(coarse_noise.at[0], noise_c, load_c.at[1]),
+            pltpu.make_async_copy(coarse_basis.at[0], basis_c, load_c.at[2]),
+        )
+
+    def fine_loads(g):
+        rows = pl.ds(pl.multiple_of(g * SUB, SUB), SUB)
+        return (
+            pltpu.make_async_copy(fine_state.at[:, rows, :], fine_next.at[:, rows, :], load_f.at[0, g]),
+            pltpu.make_async_copy(fine_noise.at[:, rows, :], noise_f.at[g], load_f.at[1, g]),
+            pltpu.make_async_copy(fine_basis.at[rows], basis_f.at[rows], load_f.at[2, g]),
+        )
+
+    def medium_loads():
+        copies = [pltpu.make_async_copy(medium_basis, basis_m, load_m.at[2 * mid_tiles])]
+        for t in range(mid_tiles):
+            cols = pl.ds(t * LANES, LANES)
+            copies.append(
+                pltpu.make_async_copy(medium_state.at[:, :, :, cols], medium_next.at[t], load_m.at[2 * t])
+            )
+            copies.append(
+                pltpu.make_async_copy(medium_noise.at[:, :, :, cols], noise_m.at[t], load_m.at[2 * t + 1])
+            )
+        return copies
+
+    for copy in coarse_loads():
+        copy.start()
+    for g in range(z.groups - 1):
+        for copy in fine_loads(g):
+            copy.start()
+    for copy in medium_loads():
+        copy.start()
+    for copy in fine_loads(z.groups - 1):
+        copy.start()
+
+    for copy in coarse_loads():
+        copy.wait()
+    mode = lax.broadcasted_iota(jnp.int32, (z.coarse, z.coarse_slots), 0)
+    degree = lax.broadcasted_iota(jnp.int32, (z.coarse, z.coarse_slots), 1)
+    inside = mode + degree < z.coarse_slots
+    planes = []
+    for c in range(2):
+        new = decay[2] * coarse_next[c] + amp[2] * noise_c[c].astype(f32)
+        new = jnp.where(inside, new, 0.0)
+        coarse_next[c] = new
+        planes.append(new)
+    planes.append(basis_c[...].astype(f32))
+    fill = jnp.zeros((32 - 3 * z.piece, z.coarse_slots), f32)
+    for p in range(lat):
+        block = [plane[p * z.piece : (p + 1) * z.piece] for plane in planes]
+        block = jnp.concatenate(block + [fill], axis=0).astype(bf16)
+        first[p] = block[:, :LANES]
+        if p < far:
+            rest = block[:, LANES:].astype(f32)
+            rest = jnp.concatenate([rest, jnp.zeros((32, 2 * LANES - z.coarse_slots), f32)], axis=1)
+            first_far[p] = rest.astype(bf16)
+
+    def first_copy(p):
+        return pltpu.make_async_remote_copy(
+            first.at[p], landed.at[a], sent_one.at[p], came_one.at[a],
+            device_id={"scale": s, "lat": p}, device_id_type=MESH,
+        )
+
+    def far_copy(p):
+        return pltpu.make_async_remote_copy(
+            first_far.at[p], landed_far.at[a], sent_far.at[p], came_far.at[a],
+            device_id={"scale": s, "lat": p}, device_id_type=MESH,
+        )
+
+    def second_copy(p):
+        return pltpu.make_async_remote_copy(
+            second.at[p], got_coarse.at[a], sent_two.at[p], came_two.at[a],
+            device_id={"scale": s, "lat": p}, device_id_type=MESH,
+        )
+
+    def row_copy(t, p):
+        return pltpu.make_async_remote_copy(
+            send.at[t, p], got.at[t, me], sent.at[t, p], came.at[t, me],
+            device_id=place(p), device_id_type=MESH,
+        )
+
+    lane = lax.broadcasted_iota(jnp.int32, (z.rows, 2 * LANES), 1) % SUB
+    shift = lax.broadcasted_iota(jnp.int32, (SUB, z.fine_slots), 0)
+    slack = z.fine_slots - me * z.fine - shift - lax.broadcasted_iota(jnp.int32, (SUB, z.fine_slots), 1)
+
+    def fine_group(g, _):
+        for copy in fine_loads(g):
+            copy.wait()
+        rows = pl.ds(pl.multiple_of(g * SUB, SUB), SUB)
+        keep = slack > g * SUB
+
+        def pair(i, _):
+            new = decay[0] * fine_next[pl.ds(2 * i, 2), rows, :] + amp[0] * noise_f[g, pl.ds(2 * i, 2)].astype(f32)
+            new = jnp.where(keep[None], new, 0.0)
+            fine_next[pl.ds(2 * i, 2), rows, :] = new
+            at = pl.ds(pl.multiple_of(2 * SUB * i, 2 * SUB), 2 * SUB)
+            half[at, :] = new.reshape(2 * SUB, z.fine_slots).astype(bf16)
+            return 0
+
+        lax.fori_loop(0, z.pairs // 2, pair, 0)
+        basis = basis_f[rows].reshape(SUB * z.rows, z.fine_slots)
+        all_pairs = lax.dot_general(basis, half[...], (((1,), (1,)), ((), ())), preferred_element_type=f32)
+        total = all_pairs[: z.rows]
+        for q in range(1, SUB):
+            total = jnp.where(lane == q, all_pairs[q * z.rows : (q + 1) * z.rows], total)
+        picked[pl.ds(pl.multiple_of(g * z.rows, z.rows), z.rows), :] = total.astype(bf16)
+        return 0
+
+    target = lax.broadcasted_iota(jnp.int32, (2 * LANES, 2 * LANES), 1)
+    wanted = (target % z.members) * (2 * SUB) + (target // z.members % 2) * SUB
+    wanted = wanted + target // LANES * 4 + target // z.pairs % 4
+    order = (lax.broadcasted_iota(jnp.int32, (2 * LANES, 2 * LANES), 0) == wanted).astype(f32).astype(bf16)
+    stride = 3 * SUB
+
+    def put_fine(g0, g1):
+        moved = jnp.dot(picked[g0 * z.rows : g1 * z.rows, :], order, preferred_element_type=f32)
+        for g in range(g0, g1):
+            for q in range(2):
+                rows_f[pl.ds(2 * g + q, z.rows, stride=stride), :] = moved[
+                    (g - g0) * z.rows : (g - g0 + 1) * z.rows, q * LANES : (q + 1) * LANES
+                ]
+
+    line = lax.broadcasted_iota(jnp.int32, (SUB, LANES), 0)
+    column = lax.broadcasted_iota(jnp.int32, (SUB, LANES), 1)
+
+    def weight(row, index):
+        at_zero = (line == row) & (column < z.pairs) & (index == 0)
+        return jnp.where(at_zero, 0.5, 1.0).astype(f32)
+
+    def ship(t):
+        scale_row = weight(0 if t == 0 else fine_quads - SUB, me)
+
+        def cast(r, _):
+            at = pl.ds(pl.multiple_of(r * stride + t * SUB, SUB), SUB)
+            send[t, r] = (rows_f[at, :].astype(bf16).astype(f32) * scale_row).astype(bf16)
+            return 0
+
+        lax.fori_loop(0, z.rows, cast, 0)
+
+        def go(i, _):
+            row_copy(t, (me + i) % n).start()
+            return 0
+
+        lax.fori_loop(1, n, go, 0)
+        got[t, me] = send[t, me]
+
+    lax.fori_loop(0, 2, fine_group, 0)
+    pl.semaphore_wait(barrier, n - 1)
+
+    def go_first(i, _):
+        p = (a + i) % lat
+        first_copy(p).start()
+
+        @pl.when(p < far)
+        def _():
+            far_copy(p).start()
+
+        return 0
+
+    lax.fori_loop(1, lat, go_first, 0)
+    landed[a] = first[a]
+
+    @pl.when(a < far)
+    def _():
+        landed_far[a] = first_far[a]
+
+    lax.fori_loop(2, z.groups - 1, fine_group, 0)
+    put_fine(0, z.groups - 1)
+    ship(0)
+
+    for copy in medium_loads():
+        copy.wait()
+    flat_next = medium_next.reshape(mid_tiles * z.pairs * z.medium, LANES)
+    flat_noise = noise_m.reshape(mid_tiles * z.pairs * z.medium, LANES)
+    span = 2 * z.medium
+    room = z.medium_slots - me * z.medium - lax.broadcasted_iota(jnp.int32, (span, LANES), 0) // 2
+    room = room - lax.broadcasted_iota(jnp.int32, (span, LANES), 1)
+
+    def medium_member(e, _):
+        for t in range(mid_tiles):
+            at = pl.ds(pl.multiple_of((t * z.members + e) * span, SUB), span)
+            new = decay[1] * flat_next[at, :] + amp[1] * flat_noise[at, :].astype(f32)
+            flat_next[at, :] = jnp.where(room > t * LANES, new, 0.0)
+        return 0
+
+    lax.fori_loop(0, z.members, medium_member, 0)
+
+    def medium_mode(m, _):
+        for c in range(2):
+            at = pl.ds(pl.multiple_of(m * z.pairs + c * z.members, z.members), z.members)
+            for t in range(mid_tiles):
+                new = flat_next[pl.ds(t * z.members * span + 2 * m + c, z.members, stride=span), :]
+                half_m[at, t * LANES : (t + 1) * LANES] = new.astype(bf16)
+        return 0
+
+    lax.fori_loop(0, z.medium, medium_mode, 0)
+    lane4 = lax.broadcasted_iota(jnp.int32, (z.rows, LANES), 1) // z.pairs
+    for q in range(medium_quads):
+        basis = basis_m[4 * q : 4 * q + 4].reshape(4 * z.rows, z.medium_slots)
+        all_pairs = lax.dot_general(
+            basis, half_m[q * LANES : (q + 1) * LANES, :], (((1,), (1,)), ((), ())), preferred_element_type=f32
+        )
+        total = all_pairs[: z.rows]
+        for b in range(1, 4):
+            total = jnp.where(lane4 == b, all_pairs[b * z.rows : (b + 1) * z.rows], total)
+        rows_f[pl.ds(fine_quads + q, z.rows, stride=stride), :] = total
+    for spare in range(fine_quads + medium_quads, 2 * SUB):
+        rows_f[pl.ds(spare, z.rows, stride=stride), :] = jnp.zeros((z.rows, LANES), f32)
+
+    lax.fori_loop(z.groups - 1, z.groups, fine_group, 0)
+    put_fine(z.groups - 1, z.groups)
+    ship(1)
+
+    def came_first(i, _):
+        p = (a + i) % lat
+        pltpu.make_async_remote_copy(
+            first.at[p], landed.at[p], sent_one.at[p], came_one.at[p],
+            device_id={"scale": s, "lat": p}, device_id_type=MESH,
+        ).wait_recv()
+        return 0
+
+    lax.fori_loop(1, lat, came_first, 0)
+    offset = (a * z.piece) % 4
+    left_c[...] = jnp.zeros_like(left_c)
+    right_c[...] = jnp.zeros_like(right_c)
+    jump = 5 * SUB
+
+    def lay(source, cols):
+        def spread(p, _):
+            landed_f[pl.ds(pl.multiple_of(p * jump, SUB), 32), :] = source[p].astype(f32)
+            return 0
+
+        lax.fori_loop(0, lat, spread, 0)
+        for i in range(z.piece):
+            for c in range(2):
+                at = pl.ds(pl.multiple_of((i + offset) * z.pairs + c * z.members, z.members), z.members)
+                values = landed_f[pl.ds(c * z.piece + i, lat, stride=jump), :]
+                right_c[at, cols] = values.astype(bf16)
+            at = pl.ds(pl.multiple_of((i + offset) * lat, lat), lat)
+            left_c[at, cols] = landed_f[pl.ds(2 * z.piece + i, lat, stride=jump), :].astype(bf16)
+
+    lay(landed, slice(0, LANES))
+
+    @pl.when(a < far)
+    def _():
+        def came_rest(i, _):
+            p = (a + i) % lat
+            pltpu.make_async_remote_copy(
+                first_far.at[0], landed_far.at[p], sent_far.at[0], came_far.at[p],
+                device_id={"scale": s, "lat": p}, device_id_type=MESH,
+            ).wait_recv()
+            return 0
+
+        lax.fori_loop(1, lat, came_rest, 0)
+        lay(landed_far, slice(LANES, 2 * LANES))
+
+    all_pairs = lax.dot_general(
+        left_c[...], right_c[...], (((1,), (1,)), ((), ())), preferred_element_type=f32
+    )
+    slot = lax.broadcasted_iota(jnp.int32, (lat, 12 * z.pairs), 1) // z.pairs
+    total = all_pairs[:lat]
+    for b in range(1, 12):
+        total = jnp.where(slot == b, all_pairs[b * lat : (b + 1) * lat], total)
+    rows_c[...] = jnp.zeros_like(rows_c)
+    for j in range(3):
+        rows_c[pl.ds(j, lat, stride=SUB), :] = total[:, j * LANES : (j + 1) * LANES]
+    scale_row = weight(0, a)
+    for p in range(lat):
+        second[p] = (rows_c[p * SUB : (p + 1) * SUB, :].astype(bf16).astype(f32) * scale_row).astype(bf16)
+
+    def go_second(i, _):
+        second_copy((a + i) % lat).start()
+        return 0
+
+    lax.fori_loop(1, lat, go_second, 0)
+    got_coarse[a] = second[a]
+
+    count = 2 * n
+    step = medium_quads * lax.broadcasted_iota(jnp.int32, (count, z.wrap), 0)
+    wave_cos[...], wave_sin[...] = turns(count, z.wrap, z.wrap, step)
+    line = lax.broadcasted_iota(jnp.int32, (SUB, z.wrap), 0)
+    cut = fine_quads - SUB
+
+    def twice(index):
+        cos, sin = turns(SUB, z.wrap, z.wrap, index)
+        return 2.0 * cos, 2.0 * sin
+
+    def turned(base, cos, sin):
+        return base[0] * cos - base[1] * sin, base[0] * sin + base[1] * cos
+
+    def keep_rows(at, upper, lower):
+        for part in range(2):
+            both = jnp.concatenate([upper[part], lower[part]], axis=0).astype(bf16)
+            for t in range(z.wrap // LANES):
+                lo = (2 * t + part) * LANES
+                table[at, lo : lo + LANES] = both[:, t * LANES : (t + 1) * LANES]
+
+    base = twice(line)
+    base_mixed = twice(jnp.where(line < cut, SUB + line, line - cut))
+    base_odd = twice(medium_quads // 2 + line)
+
+    def wave(u):
+        return wave_cos[pl.ds(u, 1), :], wave_sin[pl.ds(u, 1), :]
+
+    def fill_rows(i, _):
+        pair0, pair1 = [], []
+        for k in range(2):
+            p = 2 * i + k
+            cos, sin = wave(2 * p)
+            pair0.append(turned(base, cos, sin))
+            low_cos, low_sin = wave(p)
+            cos = jnp.where(line < cut, cos, low_cos)
+            sin = jnp.where(line < cut, sin, low_sin)
+            pair1.append(turned(base_mixed, cos, sin))
+        at = pl.multiple_of(2 * SUB * i, 2 * SUB)
+        keep_rows(pl.ds(at, 2 * SUB), *pair0)
+        keep_rows(pl.ds(at + n * SUB, 2 * SUB), *pair1)
+        return 0
+
+    lax.fori_loop(0, n // 2, fill_rows, 0)
+
+    def fill_coarse(i, _):
+        cos, sin = wave(i)
+        at = pl.multiple_of(2 * SUB * (i + n), 2 * SUB)
+        keep_rows(pl.ds(at, 2 * SUB), turned(base, cos, sin), turned(base_odd, cos, sin))
+        return 0
+
+    lax.fori_loop(0, lat // 2, fill_coarse, 0)
+
+    def came_rows(i, _):
+        p = (me + i) % n
+        for t in range(2):
+            pltpu.make_async_remote_copy(
+                send.at[t, p], got.at[t, p], sent.at[t, p], came.at[t, p],
+                device_id=place(p), device_id_type=MESH,
+            ).wait()
+        return 0
+
+    lax.fori_loop(1, n, came_rows, 0)
+
+    def came_second(i, _):
+        p = (a + i) % lat
+        pltpu.make_async_remote_copy(
+            second.at[p], got_coarse.at[p], sent_two.at[p], came_two.at[p],
+            device_id={"scale": s, "lat": p}, device_id_type=MESH,
+        ).wait()
+        first_copy(p).wait_send()
+
+        @pl.when(p < far)
+        def _():
+            far_copy(p).wait_send()
+
+        return 0
+
+    lax.fori_loop(1, lat, came_second, 0)
+
+
+def grid_kernel(
+    z, fine_in, medium_in, coarse_in, got, got_coarse, table, fine_out, medium_out, coarse_out, out, turned, sems
+):
+    copies = [
+        pltpu.make_async_copy(fine_in, fine_out, sems.at[0]),
+        pltpu.make_async_copy(coarse_in, coarse_out.at[0], sems.at[1]),
+    ]
+    for t in range(medium_in.shape[0]):
+        cols = pl.ds(t * LANES, LANES)
+        copies.append(pltpu.make_async_copy(medium_in.at[t], medium_out.at[:, :, :, cols], sems.at[2 + t]))
+    for copy in copies:
+        copy.start()
+    many = 2 * z.n * SUB
+    turned[:, :many] = got[...].reshape(many, LANES).astype(jnp.float32).T.astype(jnp.bfloat16)
+    few = got_coarse[...].reshape(z.lat * SUB, LANES).astype(jnp.float32)
+    turned[:, many:] = few.T.astype(jnp.bfloat16)
+    e, tiles = z.members, z.wrap // LANES
+    for t in range(tiles):
+        both = jnp.dot(turned[...], table[:, 2 * t * LANES : 2 * (t + 1) * LANES], preferred_element_type=jnp.float32)
+        waves = []
+        for b in range(4):
+            at = 2 * b * e
+            cos_r, sin_r = both[at : at + e, :LANES], both[at : at + e, LANES:]
+            cos_i, sin_i = both[at + e : at + 2 * e, :LANES], both[at + e : at + 2 * e, LANES:]
+            re, im = cos_r - sin_i, sin_r + cos_i
+            if b:
+                angle = (lax.broadcasted_iota(jnp.int32, (1, LANES), 1) + t * LANES).astype(jnp.float32)
+                angle = angle * (2.0 * math.pi * b / NLON)
+                cos, sin = jnp.cos(angle), jnp.sin(angle)
+                re, im = re * cos - im * sin, re * sin + im * cos
+            waves.append((re, im))
+        for h in range(4):
+            total = None
+            for b in range(4):
+                re, im = waves[b]
+                term = (re, -im, -re, im)[b * h % 4]
+                total = term if total is None else total + term
+            out[pl.ds(h * tiles + t, e, stride=4 * tiles), :] = jnp.tanh(total)
+    for copy in copies:
+        copy.wait()
+
+
+def fast_body(
+    z,
+    fine_state,
+    fine_noise,
+    medium_state,
+    medium_noise,
+    coarse_state,
+    coarse_noise,
+    decay,
+    amplitude,
+    fine_basis,
+    medium_basis,
+    coarse_basis,
+):
+    f32, bf16, dma = jnp.float32, jnp.bfloat16, pltpu.SemaphoreType.DMA
+    e, n, lat, rows = z.members, z.n, z.lat, z.rows
+    tiles = z.medium_slots // LANES
+    far = -(-(z.coarse_slots - LANES) // z.piece)
+    table_rows = (2 * n + lat) * SUB
+    operands = (
+        fine_state.reshape(z.pairs, z.fine, z.fine_slots),
+        fine_noise.reshape(z.pairs, z.fine, z.fine_slots),
+        fine_basis,
+        medium_state.transpose(0, 2, 1, 3),
+        medium_noise.transpose(0, 2, 1, 3),
+        medium_basis,
+        coarse_state,
+        coarse_noise,
+        coarse_basis,
+    )
+    operands = tuple(pltpu.with_memory_space_constraint(x, pltpu.HBM) for x in operands)
+    vmem = pl.BlockSpec(memory_space=pltpu.VMEM)
+    hbm = pl.BlockSpec(memory_space=pltpu.HBM)
+    smem = pl.BlockSpec(memory_space=pltpu.SMEM)
+    between = (
+        pltpu.VMEM((z.pairs, z.fine, z.fine_slots), f32),
+        pltpu.VMEM((tiles, e, z.medium, 2, LANES), f32),
+        pltpu.VMEM((2, z.coarse, z.coarse_slots), f32),
+        pltpu.VMEM((2, n, SUB, LANES), bf16),
+        pltpu.VMEM((lat, SUB, LANES), bf16),
+        pltpu.VMEM((table_rows, 2 * z.wrap), bf16),
+    )
+    held = pl.pallas_call(
+        functools.partial(spread_kernel, z),
+        out_shape=between,
+        in_specs=[smem, smem] + [hbm] * 9,
+        out_specs=(vmem,) * 6,
+        scratch_shapes=[
+            pltpu.VMEM((z.groups, z.pairs, SUB, z.fine_slots), bf16),
+            pltpu.VMEM((z.fine, rows, z.fine_slots), bf16),
+            pltpu.VMEM((SUB * z.pairs, z.fine_slots), bf16),
+            pltpu.VMEM((z.groups * rows, 2 * LANES), bf16),
+            pltpu.VMEM((tiles, e, z.medium, 2, LANES), bf16),
+            pltpu.VMEM((z.medium, rows, z.medium_slots), bf16),
+            pltpu.VMEM((z.medium * z.pairs, z.medium_slots), bf16),
+            pltpu.VMEM((rows * 3 * SUB, LANES), f32),
+            pltpu.VMEM((2, n, SUB, LANES), bf16),
+            pltpu.VMEM((2, z.coarse, z.coarse_slots), bf16),
+            pltpu.VMEM((z.coarse, z.coarse_slots), bf16),
+            pltpu.VMEM((lat, 32, LANES), bf16),
+            pltpu.VMEM((far, 32, LANES), bf16),
+            pltpu.VMEM((lat, 32, LANES), bf16),
+            pltpu.VMEM((lat, 32, LANES), bf16),
+            pltpu.VMEM((lat * 5 * SUB, LANES), f32),
+            pltpu.VMEM((12 * lat, 2 * LANES), bf16),
+            pltpu.VMEM((12 * z.pairs, 2 * LANES), bf16),
+            pltpu.VMEM((lat * SUB, LANES), f32),
+            pltpu.VMEM((lat, SUB, LANES), bf16),
+            pltpu.VMEM((2 * n, z.wrap), f32),
+            pltpu.VMEM((2 * n, z.wrap), f32),
+            dma((3, z.groups)),
+            dma((2 * tiles + 1,)),
+            dma((3,)),
+            dma((2, n)),
+            dma((2, n)),
+            dma((lat,)),
+            dma((lat,)),
+            dma((lat,)),
+            dma((lat,)),
+            dma((lat,)),
+            dma((lat,)),
+        ],
+        compiler_params=pltpu.CompilerParams(
+            collective_id=0, has_side_effects=True, vmem_limit_bytes=32 * 1024 * 1024
+        ),
+    )(decay, amplitude, *operands)
+    fine_next, medium_next, coarse_next, pattern = pl.pallas_call(
+        functools.partial(grid_kernel, z),
+        out_shape=(
+            jax.ShapeDtypeStruct((z.pairs, z.fine, z.fine_slots), f32),
+            jax.ShapeDtypeStruct((e, z.medium, 2, z.medium_slots), f32),
+            jax.ShapeDtypeStruct(coarse_state.shape, f32),
+            jax.ShapeDtypeStruct((e * NLON // LANES, LANES), f32),
+        ),
+        in_specs=[vmem] * 6,
+        out_specs=(hbm, hbm, hbm, vmem),
+        scratch_shapes=[pltpu.VMEM((LANES, table_rows), bf16), dma((2 + tiles,))],
+        compiler_params=pltpu.CompilerParams(vmem_limit_bytes=32 * 1024 * 1024),
+    )(*held)
+    return (
+        fine_next.reshape(fine_state.shape),
+        medium_next.transpose(0, 2, 1, 3),
+        coarse_next,
+        pattern.reshape(e, 1, NLON),
+    )
+
+
+def body(*arrays):
+    fine_state, medium_state, coarse_state = arrays[0], arrays[2], arrays[4]
+    scale, lat = lax.axis_size("scale"), lax.axis_size("lat")
+    z = Sizes(fine_state, medium_state, coarse_state, arrays[8], arrays[10], scale, lat)
+    return fast_body(z, *arrays) if z.fits() else general_body(*arrays)
+
+
 def solution(mesh):
     return jax.shard_map(
         body,

time: 54.9 us -> 32.2 us (0.59)
  Pallas kernels: 9.46 us -> 30.1 us
  other arithmetic: 13.3 us -> 0 us
  starting transfers between devices: 13.2 us -> 0 us
  local copies, waits for them, and re-layouts: 8.99 us -> 1.3 us
  waiting for transfers between devices: 4.78 us -> 0 us
  matrix products: 3.94 us -> 0 us
    pallas_call x3 -> x2, Pallas kernels: 9.46 us -> 30.1 us  [the longest x1 25.8 us: fast_body(): pl.pallas_call(functools.partial(spread_kernel, z), out_shape=between, in...]
    all_to_all x2 -> x0, starting transfers between devices: 13.2 us -> none  [the longest x1 7.33 us: body(): lax.all_to_all(mixed, ('scale', 'lat'), split_axis=0, concat_axis=0, tile...]
    convert_element_type x2 -> x0, other arithmetic: 10.7 us -> none  [the longest x1 7.86 us: body(): fine_next.astype(jnp.bfloat16)]
    all_to_all x2 -> x0, waiting for transfers between devices: 4.78 us -> none  [the longest x1 4.78 us: body(): lax.all_to_all(both, ('scale', 'lat'), split_axis=0, concat_axis=0, tiled...]
    dot_general x3 -> x0, matrix products: 3.94 us -> none  [body(): jnp.einsum(form, half, basis, preferred_element_type=jnp.float32)]
    reshape x3 -> x0, local copies, waits for them, and re-layouts: 3.55 us -> none  [phase_blocks(): return fourier.reshape(rows, parts * high, FOLD * members)]
    convert_element_type x2 -> x0, local copies, waits for them, and re-layouts: 2.42 us -> none  [body(): jnp.einsum(form, half, basis, preferred_element_type=jnp.float32)]
    slice x2 -> x0, local copies, waits for them, and re-layouts: 2.19 us -> none  [the longest x1 1.38 us: body(): medium_rates[0]]
  transfers between devices with their start and end apart: 2 -> 0, of which waited for: 1 -> 0; matrix products, arithmetic and copies ran while one was open for 43% -> 0% of each run, Pallas kernels for 8% -> 0%
where the time goes in v1:
time: 32.2 us; the launch traced here: 32.1 us
  Pallas kernels  30.1 us (93%)
  local copies, waits for them, and re-layouts  1.3 us (4%)
  between operations  0.65 us (2%)
    pallas_call x1, Pallas kernels, fast_body(): pl.pallas_call(functools.partial(spread_kernel, z), out_shape=between, in...  25.8 us
    pallas_call x1, Pallas kernels, fast_body(): pl.pallas_call(functools.partial(grid_kernel, z), out_shape=(jax.ShapeDty...  4.32 us
    unnamed x4, local copies, waits for them, and re-layouts  1.3 us

profile of v1, /device:TPU:0, one launch (start us, length us, event | category | flops | bytes accessed | tf_op | source)
XLA Modules:
  0.0 32.1 jit_solution(16093901325318432147)
XLA Ops:
  0.6 0.0 copy-start
  0.6 0.6 %copy-done = f32[3]{0:T(128)S(1)} copy-done((f32[3]{0:T(128)S(1)}, f32[3]{0:T(128)}, u32[]{:S(2)}) %copy-start) | copy-done | bytes 36
  1.3 0.0 copy-start.1
  1.3 0.7 %copy-done.1 = f32[3]{0:T(128)S(1)} copy-done((f32[3]{0:T(128)S(1)}, f32[3]{0:T(128)}, u32[]{:S(2)}) %copy-start.1) | copy-done | bytes 36
  1.9 25.8 %shard_map.138 = (f32[32,40,1280]{2,1,0:T(8,128)S(1)}, f32[5,16,20,2,128]{4,3,2,1,0:T(2,128)S(1)}, f32[2,160,160]{2,1,0:T(8,128)S(1)}, bf16[2,32,8,128]{3,2,1,0:...) custom-call(f32[3]{0:T(128)S(1)} %copy-done, f32[3]{0:T(128)S(1)} %copy-done.1, ...), custom_call_target="tpu_custom_call" | custom-call | tf_op jit(solution)/shard_map/pallas_call | solution.py:771
  27.8 4.3 %shard_map.139 = (f32[32,40,1280]{2,1,0:T(8,128)}, f32[16,20,2,640]{3,2,1,0:T(2,128)}, f32[1,2,160,160]{3,2,1,0:T(8,128)}, f32[320,128]{1,0:T(8,128)}) custom-call(f32[32,40,1280]{2,1,0:T(8,128)S(1)} %get-tuple-element.14.fine_in, f32[5,16,20,2,128]{4,3,2,1,0:T(2,128)S(1)} %get-tuple-element.15.medium_in, f32[2,160,160]{2,1,0:T(8,128)S(1)} %get-tuple-element.16.coarse_in, ...), custom_call_target="tpu_custom_call" | custom-call | tf_op jit(solution)/shard_map/pallas_call | solution.py:815
Async XLA Ops:
  0.6 0.7 %copy-start = (f32[3]{0:T(128)S(1)}, f32[3]{0:T(128)}, u32[]{:S(2)}) copy-start(f32[3]{0:T(128)} %decay.1) | copy-start | bytes 40
  1.3 0.7 %copy-start.1 = (f32[3]{0:T(128)S(1)}, f32[3]{0:T(128)}, u32[]{:S(2)}) copy-start(f32[3]{0:T(128)} %amp.1) | copy-start | bytes 40

commit v2 on v1

--- a/solution.py
+++ b/solution.py
@@ -239,9 +239,10 @@
             return False
         if self.fine_slots % LANES or self.medium_slots % LANES or self.coarse % self.lat:
             return False
-        if self.piece != 2 * (self.medium // 4) or 3 * self.piece > 32 or self.piece + 2 > 12:
+        over = self.coarse_slots - LANES
+        if self.coarse_slots != self.coarse or over <= 0 or 2 * over > LANES or over % self.lat:
             return False
-        if not LANES < self.coarse_slots <= 2 * LANES or self.coarse_slots != self.coarse:
+        if 3 * self.piece > 32 or self.lat % 4 or LANES * self.pairs // self.lat % LANES:
             return False
         high = self.fine // 4
         return SUB <= high and high - SUB + self.medium // 4 <= SUB and self.wrap % LANES == 0
@@ -255,8 +256,8 @@
 
 def spread_kernel(
     z,
-    decay,
-    amp,
+    decay_in,
+    amp_in,
     fine_state,
     fine_noise,
     fine_basis,
@@ -283,28 +284,22 @@
     send,
     noise_c,
     basis_c,
+    spread,
     first,
-    first_far,
     landed,
-    landed_far,
     landed_f,
     left_c,
     right_c,
-    rows_c,
     second,
     wave_cos,
     wave_sin,
+    decay,
+    amp,
     load_f,
     load_m,
     load_c,
     sent,
     came,
-    sent_one,
-    came_one,
-    sent_far,
-    came_far,
-    sent_two,
-    came_two,
 ):
     n, lat = z.n, z.lat
     s, a = lax.axis_index("scale"), lax.axis_index("lat")
@@ -312,7 +307,8 @@
     f32, bf16 = jnp.float32, jnp.bfloat16
     mid_tiles = z.medium_slots // LANES
     fine_quads, medium_quads = z.fine // 4, z.medium // 4
-    far = -(-(z.coarse_slots - LANES) // z.piece)
+    over = z.coarse_slots - LANES
+    stride, pitch = 3 * SUB, 3 * SUB
 
     def place(p):
         return {"scale": p // lat, "lat": p % lat}
@@ -327,84 +323,86 @@
 
     def coarse_loads():
         return (
-            pltpu.make_async_copy(coarse_state.at[0], coarse_next, load_c.at[0]),
-            pltpu.make_async_copy(coarse_noise.at[0], noise_c, load_c.at[1]),
-            pltpu.make_async_copy(coarse_basis.at[0], basis_c, load_c.at[2]),
+            pltpu.make_async_copy(decay_in, decay, load_c),
+            pltpu.make_async_copy(amp_in, amp, load_c),
+            pltpu.make_async_copy(coarse_state.at[0], coarse_next, load_c),
+            pltpu.make_async_copy(coarse_noise.at[0], noise_c, load_c),
+            pltpu.make_async_copy(coarse_basis.at[0], basis_c, load_c),
         )
 
     def fine_loads(g):
         rows = pl.ds(pl.multiple_of(g * SUB, SUB), SUB)
         return (
-            pltpu.make_async_copy(fine_state.at[:, rows, :], fine_next.at[:, rows, :], load_f.at[0, g]),
-            pltpu.make_async_copy(fine_noise.at[:, rows, :], noise_f.at[g], load_f.at[1, g]),
-            pltpu.make_async_copy(fine_basis.at[rows], basis_f.at[rows], load_f.at[2, g]),
+            pltpu.make_async_copy(fine_state.at[:, rows, :], fine_next.at[:, rows, :], load_f.at[g]),
+            pltpu.make_async_copy(fine_noise.at[:, rows, :], noise_f.at[g], load_f.at[g]),
+            pltpu.make_async_copy(fine_basis.at[rows], basis_f.at[rows], load_f.at[g]),
         )
 
     def medium_loads():
-        copies = [pltpu.make_async_copy(medium_basis, basis_m, load_m.at[2 * mid_tiles])]
+        copies = [pltpu.make_async_copy(medium_basis, basis_m, load_m)]
         for t in range(mid_tiles):
             cols = pl.ds(t * LANES, LANES)
             copies.append(
-                pltpu.make_async_copy(medium_state.at[:, :, :, cols], medium_next.at[t], load_m.at[2 * t])
+                pltpu.make_async_copy(medium_state.at[:, :, :, cols], medium_next.at[t], load_m)
             )
             copies.append(
-                pltpu.make_async_copy(medium_noise.at[:, :, :, cols], noise_m.at[t], load_m.at[2 * t + 1])
+                pltpu.make_async_copy(medium_noise.at[:, :, :, cols], noise_m.at[t], load_m)
             )
         return copies
 
-    for copy in coarse_loads():
-        copy.start()
-    for g in range(z.groups - 1):
-        for copy in fine_loads(g):
+    def start(copies):
+        for copy in copies:
             copy.start()
-    for copy in medium_loads():
-        copy.start()
-    for copy in fine_loads(z.groups - 1):
-        copy.start()
-
-    for copy in coarse_loads():
-        copy.wait()
-    mode = lax.broadcasted_iota(jnp.int32, (z.coarse, z.coarse_slots), 0)
-    degree = lax.broadcasted_iota(jnp.int32, (z.coarse, z.coarse_slots), 1)
-    inside = mode + degree < z.coarse_slots
-    planes = []
-    for c in range(2):
-        new = decay[2] * coarse_next[c] + amp[2] * noise_c[c].astype(f32)
-        new = jnp.where(inside, new, 0.0)
-        coarse_next[c] = new
-        planes.append(new)
-    planes.append(basis_c[...].astype(f32))
-    fill = jnp.zeros((32 - 3 * z.piece, z.coarse_slots), f32)
-    for p in range(lat):
-        block = [plane[p * z.piece : (p + 1) * z.piece] for plane in planes]
-        block = jnp.concatenate(block + [fill], axis=0).astype(bf16)
-        first[p] = block[:, :LANES]
-        if p < far:
-            rest = block[:, LANES:].astype(f32)
-            rest = jnp.concatenate([rest, jnp.zeros((32, 2 * LANES - z.coarse_slots), f32)], axis=1)
-            first_far[p] = rest.astype(bf16)
-
-    def first_copy(p):
+
+    @jax.named_scope("advance_coarse")
+    def advance_coarse():
+        with jax.named_scope("wait_coarse"):
+            for copy in coarse_loads():
+                copy.wait()
+        mode = lax.broadcasted_iota(jnp.int32, (z.coarse, z.coarse_slots), 0)
+        degree = lax.broadcasted_iota(jnp.int32, (z.coarse, z.coarse_slots), 1)
+        inside = mode + degree < z.coarse_slots
+        planes = []
+        for c in range(2):
+            new = decay[2] * coarse_next[c] + amp[2] * noise_c[c].astype(f32)
+            new = jnp.where(inside, new, 0.0)
+            coarse_next[c] = new
+            planes.append(new)
+        planes.append(basis_c[...].astype(f32))
+        column_c = lax.broadcasted_iota(jnp.int32, (lat, LANES), 1)
+        for k, plane in enumerate(planes):
+            rest = plane[:over, LANES:]
+            rest = jnp.concatenate([jnp.zeros_like(rest), rest, jnp.zeros((over, LANES - 2 * over), f32)], axis=1)
+            for i in range(z.piece):
+                rows = plane[i * lat : (i + 1) * lat, :LANES]
+                low = i * lat - LANES
+                if low >= 0:
+                    rows = jnp.where(column_c < over, rows, rest[low : low + lat])
+                spread[pl.ds((3 * i + k) * pitch, lat), :] = rows
+        for p in range(lat):
+            first[p] = spread[pl.ds(p, 32, stride=pitch), :].astype(bf16)
+
+    def first_copy(p, count=None):
+        at = p if count is None else pl.ds(p, count)
+        to = a if count is None else at
         return pltpu.make_async_remote_copy(
-            first.at[p], landed.at[a], sent_one.at[p], came_one.at[a],
+            first.at[at], landed.at[to], sent.at[0], came.at[0],
             device_id={"scale": s, "lat": p}, device_id_type=MESH,
         )
 
-    def far_copy(p):
+    def second_copy(p, count=None):
+        at = p if count is None else pl.ds(p, count)
+        to = a if count is None else at
         return pltpu.make_async_remote_copy(
-            first_far.at[p], landed_far.at[a], sent_far.at[p], came_far.at[a],
+            second.at[at], got_coarse.at[to], sent.at[1], came.at[1],
             device_id={"scale": s, "lat": p}, device_id_type=MESH,
         )
 
-    def second_copy(p):
+    def row_copy(p, count=None):
+        at = p if count is None else pl.ds(p, count)
+        to = me if count is None else at
         return pltpu.make_async_remote_copy(
-            second.at[p], got_coarse.at[a], sent_two.at[p], came_two.at[a],
-            device_id={"scale": s, "lat": p}, device_id_type=MESH,
-        )
-
-    def row_copy(t, p):
-        return pltpu.make_async_remote_copy(
-            send.at[t, p], got.at[t, me], sent.at[t, p], came.at[t, me],
+            send.at[at], got.at[to], sent.at[2], came.at[2],
             device_id=place(p), device_id_type=MESH,
         )
 
@@ -412,6 +410,7 @@
     shift = lax.broadcasted_iota(jnp.int32, (SUB, z.fine_slots), 0)
     slack = z.fine_slots - me * z.fine - shift - lax.broadcasted_iota(jnp.int32, (SUB, z.fine_slots), 1)
 
+    @jax.named_scope("fine_group")
     def fine_group(g, _):
         for copy in fine_loads(g):
             copy.wait()
@@ -439,8 +438,7 @@
     wanted = (target % z.members) * (2 * SUB) + (target // z.members % 2) * SUB
     wanted = wanted + target // LANES * 4 + target // z.pairs % 4
     order = (lax.broadcasted_iota(jnp.int32, (2 * LANES, 2 * LANES), 0) == wanted).astype(f32).astype(bf16)
-    stride = 3 * SUB
-
+    @jax.named_scope("put_fine")
     def put_fine(g0, g1):
         moved = jnp.dot(picked[g0 * z.rows : g1 * z.rows, :], order, preferred_element_type=f32)
         for g in range(g0, g1):
@@ -456,159 +454,125 @@
         at_zero = (line == row) & (column < z.pairs) & (index == 0)
         return jnp.where(at_zero, 0.5, 1.0).astype(f32)
 
-    def ship(t):
-        scale_row = weight(0 if t == 0 else fine_quads - SUB, me)
+    @jax.named_scope("ship")
+    def ship():
+        scale_row = jnp.concatenate([weight(0, me), weight(fine_quads - SUB, me)], axis=0)
 
         def cast(r, _):
-            at = pl.ds(pl.multiple_of(r * stride + t * SUB, SUB), SUB)
-            send[t, r] = (rows_f[at, :].astype(bf16).astype(f32) * scale_row).astype(bf16)
+            at = pl.ds(pl.multiple_of(r * stride, SUB), 2 * SUB)
+            send[r] = (rows_f[at, :].astype(bf16).astype(f32) * scale_row).astype(bf16)
             return 0
 
-        lax.fori_loop(0, z.rows, cast, 0)
-
-        def go(i, _):
-            row_copy(t, (me + i) % n).start()
+        lax.fori_loop(0, z.rows, cast, 0, unroll=4)
+        for i in range(1, n):
+            row_copy((me + i) % n).start()
+        got[me] = send[me]
+
+    @jax.named_scope("send_first")
+    def send_first():
+        for i in range(1, lat):
+            first_copy((a + i) % lat).start()
+        landed[a] = first[a]
+
+    @jax.named_scope("medium_rows")
+    def medium_rows():
+        for copy in medium_loads():
+            copy.wait()
+        flat_next = medium_next.reshape(mid_tiles * z.pairs * z.medium, LANES)
+        flat_noise = noise_m.reshape(mid_tiles * z.pairs * z.medium, LANES)
+        span = 2 * z.medium
+        room = z.medium_slots - me * z.medium - lax.broadcasted_iota(jnp.int32, (span, LANES), 0) // 2
+        room = room - lax.broadcasted_iota(jnp.int32, (span, LANES), 1)
+
+        def medium_member(e, _):
+            for t in range(mid_tiles):
+                at = pl.ds(pl.multiple_of((t * z.members + e) * span, SUB), span)
+                new = decay[1] * flat_next[at, :] + amp[1] * flat_noise[at, :].astype(f32)
+                flat_next[at, :] = jnp.where(room > t * LANES, new, 0.0)
             return 0
 
-        lax.fori_loop(1, n, go, 0)
-        got[t, me] = send[t, me]
-
-    lax.fori_loop(0, 2, fine_group, 0)
-    pl.semaphore_wait(barrier, n - 1)
-
-    def go_first(i, _):
-        p = (a + i) % lat
-        first_copy(p).start()
-
-        @pl.when(p < far)
-        def _():
-            far_copy(p).start()
-
-        return 0
-
-    lax.fori_loop(1, lat, go_first, 0)
-    landed[a] = first[a]
-
-    @pl.when(a < far)
-    def _():
-        landed_far[a] = first_far[a]
-
-    lax.fori_loop(2, z.groups - 1, fine_group, 0)
-    put_fine(0, z.groups - 1)
-    ship(0)
-
-    for copy in medium_loads():
-        copy.wait()
-    flat_next = medium_next.reshape(mid_tiles * z.pairs * z.medium, LANES)
-    flat_noise = noise_m.reshape(mid_tiles * z.pairs * z.medium, LANES)
-    span = 2 * z.medium
-    room = z.medium_slots - me * z.medium - lax.broadcasted_iota(jnp.int32, (span, LANES), 0) // 2
-    room = room - lax.broadcasted_iota(jnp.int32, (span, LANES), 1)
-
-    def medium_member(e, _):
-        for t in range(mid_tiles):
-            at = pl.ds(pl.multiple_of((t * z.members + e) * span, SUB), span)
-            new = decay[1] * flat_next[at, :] + amp[1] * flat_noise[at, :].astype(f32)
-            flat_next[at, :] = jnp.where(room > t * LANES, new, 0.0)
-        return 0
-
-    lax.fori_loop(0, z.members, medium_member, 0)
-
-    def medium_mode(m, _):
-        for c in range(2):
-            at = pl.ds(pl.multiple_of(m * z.pairs + c * z.members, z.members), z.members)
-            for t in range(mid_tiles):
-                new = flat_next[pl.ds(t * z.members * span + 2 * m + c, z.members, stride=span), :]
-                half_m[at, t * LANES : (t + 1) * LANES] = new.astype(bf16)
-        return 0
-
-    lax.fori_loop(0, z.medium, medium_mode, 0)
-    lane4 = lax.broadcasted_iota(jnp.int32, (z.rows, LANES), 1) // z.pairs
-    for q in range(medium_quads):
-        basis = basis_m[4 * q : 4 * q + 4].reshape(4 * z.rows, z.medium_slots)
-        all_pairs = lax.dot_general(
-            basis, half_m[q * LANES : (q + 1) * LANES, :], (((1,), (1,)), ((), ())), preferred_element_type=f32
-        )
-        total = all_pairs[: z.rows]
-        for b in range(1, 4):
-            total = jnp.where(lane4 == b, all_pairs[b * z.rows : (b + 1) * z.rows], total)
-        rows_f[pl.ds(fine_quads + q, z.rows, stride=stride), :] = total
-    for spare in range(fine_quads + medium_quads, 2 * SUB):
-        rows_f[pl.ds(spare, z.rows, stride=stride), :] = jnp.zeros((z.rows, LANES), f32)
-
-    lax.fori_loop(z.groups - 1, z.groups, fine_group, 0)
-    put_fine(z.groups - 1, z.groups)
-    ship(1)
-
-    def came_first(i, _):
-        p = (a + i) % lat
-        pltpu.make_async_remote_copy(
-            first.at[p], landed.at[p], sent_one.at[p], came_one.at[p],
-            device_id={"scale": s, "lat": p}, device_id_type=MESH,
-        ).wait_recv()
-        return 0
-
-    lax.fori_loop(1, lat, came_first, 0)
-    offset = (a * z.piece) % 4
-    left_c[...] = jnp.zeros_like(left_c)
-    right_c[...] = jnp.zeros_like(right_c)
-    jump = 5 * SUB
-
-    def lay(source, cols):
-        def spread(p, _):
-            landed_f[pl.ds(pl.multiple_of(p * jump, SUB), 32), :] = source[p].astype(f32)
+        lax.fori_loop(0, z.members, medium_member, 0)
+
+        def medium_mode(m, _):
+            for c in range(2):
+                at = pl.ds(pl.multiple_of(m * z.pairs + c * z.members, z.members), z.members)
+                for t in range(mid_tiles):
+                    new = flat_next[pl.ds(t * z.members * span + 2 * m + c, z.members, stride=span), :]
+                    half_m[at, t * LANES : (t + 1) * LANES] = new.astype(bf16)
             return 0
 
-        lax.fori_loop(0, lat, spread, 0)
+        lax.fori_loop(0, z.medium, medium_mode, 0)
+        lane4 = lax.broadcasted_iota(jnp.int32, (z.rows, LANES), 1) // z.pairs
+        for q in range(medium_quads):
+            basis = basis_m[4 * q : 4 * q + 4].reshape(4 * z.rows, z.medium_slots)
+            all_pairs = lax.dot_general(
+                basis, half_m[q * LANES : (q + 1) * LANES, :], (((1,), (1,)), ((), ())), preferred_element_type=f32
+            )
+            total = all_pairs[: z.rows]
+            for b in range(1, 4):
+                total = jnp.where(lane4 == b, all_pairs[b * z.rows : (b + 1) * z.rows], total)
+            rows_f[pl.ds(fine_quads + q, z.rows, stride=stride), :] = total
+        for spare in range(fine_quads + medium_quads, 2 * SUB):
+            rows_f[pl.ds(spare, z.rows, stride=stride), :] = jnp.zeros((z.rows, LANES), f32)
+
+    @jax.named_scope("wait_first")
+    def wait_first():
+        first_copy(0, lat - 1).wait()
+
+    @jax.named_scope("coarse_rows")
+    def coarse_rows():
+        jump = 5 * SUB
+
+        def widen(p, _):
+            landed_f[pl.ds(pl.multiple_of(p * jump, SUB), 32), :] = landed[p].astype(f32)
+            return 0
+
+        lax.fori_loop(0, lat, widen, 0, unroll=4)
+        lane = lax.broadcasted_iota(jnp.int32, (lat, LANES), 1)
+        shared = LANES // lat
         for i in range(z.piece):
             for c in range(2):
-                at = pl.ds(pl.multiple_of((i + offset) * z.pairs + c * z.members, z.members), z.members)
-                values = landed_f[pl.ds(c * z.piece + i, lat, stride=jump), :]
-                right_c[at, cols] = values.astype(bf16)
-            at = pl.ds(pl.multiple_of((i + offset) * lat, lat), lat)
-            left_c[at, cols] = landed_f[pl.ds(2 * z.piece + i, lat, stride=jump), :].astype(bf16)
-
-    lay(landed, slice(0, LANES))
-
-    @pl.when(a < far)
-    def _():
-        def came_rest(i, _):
-            p = (a + i) % lat
-            pltpu.make_async_remote_copy(
-                first_far.at[0], landed_far.at[p], sent_far.at[0], came_far.at[p],
-                device_id={"scale": s, "lat": p}, device_id_type=MESH,
-            ).wait_recv()
-            return 0
-
-        lax.fori_loop(1, lat, came_rest, 0)
-        lay(landed_far, slice(LANES, 2 * LANES))
-
-    all_pairs = lax.dot_general(
-        left_c[...], right_c[...], (((1,), (1,)), ((), ())), preferred_element_type=f32
-    )
-    slot = lax.broadcasted_iota(jnp.int32, (lat, 12 * z.pairs), 1) // z.pairs
-    total = all_pairs[:lat]
-    for b in range(1, 12):
-        total = jnp.where(slot == b, all_pairs[b * lat : (b + 1) * lat], total)
-    rows_c[...] = jnp.zeros_like(rows_c)
-    for j in range(3):
-        rows_c[pl.ds(j, lat, stride=SUB), :] = total[:, j * LANES : (j + 1) * LANES]
-    scale_row = weight(0, a)
-    for p in range(lat):
-        second[p] = (rows_c[p * SUB : (p + 1) * SUB, :].astype(bf16).astype(f32) * scale_row).astype(bf16)
-
-    def go_second(i, _):
-        second_copy((a + i) % lat).start()
-        return 0
-
-    lax.fori_loop(1, lat, go_second, 0)
-    got_coarse[a] = second[a]
-
-    count = 2 * n
-    step = medium_quads * lax.broadcasted_iota(jnp.int32, (count, z.wrap), 0)
-    wave_cos[...], wave_sin[...] = turns(count, z.wrap, z.wrap, step)
-    line = lax.broadcasted_iota(jnp.int32, (SUB, z.wrap), 0)
-    cut = fine_quads - SUB
+                values = landed_f[pl.ds(3 * i + c, lat, stride=jump), :]
+                right_c[i * z.pairs + c * z.members : i * z.pairs + (c + 1) * z.members, :] = values.astype(bf16)
+            values = landed_f[pl.ds(3 * i + 2, lat, stride=jump), :]
+            if i >= shared:
+                extra = jnp.where(lane >= over, values, 0.0)
+                values = jnp.where(lane < over, values, 0.0)
+                left_c[(z.piece + i - shared) * lat : (z.piece + i - shared + 1) * lat, :] = extra.astype(bf16)
+            left_c[i * lat : (i + 1) * lat, :] = values.astype(bf16)
+        all_pairs = lax.dot_general(
+            left_c[...], right_c[...], (((1,), (1,)), ((), ())), preferred_element_type=f32
+        )
+        slot = lax.broadcasted_iota(jnp.int32, (lat, z.piece * z.pairs), 1) // z.pairs
+        total = all_pairs[:lat]
+        for i in range(1, z.piece):
+            total = jnp.where(slot == i, all_pairs[i * lat : (i + 1) * lat], total)
+        extra = all_pairs[z.piece * lat : (z.piece + 1) * lat]
+        for i in range(shared + 1, z.piece):
+            extra = jnp.where(slot == i, all_pairs[(z.piece + i - shared) * lat : (z.piece + i - shared + 1) * lat], extra)
+        block = lane // z.pairs
+        for i in range(z.piece):
+            j = i // 4
+            row = total[:, j * LANES : min((j + 1) * LANES, total.shape[1])]
+            if i < z.piece - shared:
+                far = extra[:, shared * z.pairs + j * LANES :]
+                row = row + jnp.concatenate([far, jnp.zeros((lat, LANES - far.shape[1]), f32)], axis=1)
+            if row.shape[1] < LANES:
+                row = jnp.concatenate([row, jnp.zeros((lat, LANES - row.shape[1]), f32)], axis=1)
+            row = pltpu.roll(row, ((a % 4 - i % 4 + 4) % 4) * z.pairs, axis=1)
+            spread[pl.ds(i, lat, stride=pitch), :] = jnp.where(block == a % 4, row, 0.0)
+        for i in range(z.piece, 2 * SUB):
+            spread[pl.ds(i, lat, stride=pitch), :] = jnp.zeros((lat, LANES), f32)
+        scale_row = jnp.concatenate([weight(0, a), jnp.ones((SUB, LANES), f32)], axis=0)
+        for p in range(lat):
+            rows = spread[p * pitch : p * pitch + 2 * SUB, :].astype(bf16).astype(f32)
+            second[p] = (rows * scale_row).astype(bf16)
+        for i in range(1, lat):
+            second_copy((a + i) % lat).start()
+        got_coarse[a] = second[a]
+
+    line_t = lax.broadcasted_iota(jnp.int32, (SUB, z.wrap), 0)
+    left_over = fine_quads - SUB
 
     def twice(index):
         cos, sin = turns(SUB, z.wrap, z.wrap, index)
@@ -624,64 +588,74 @@
                 lo = (2 * t + part) * LANES
                 table[at, lo : lo + LANES] = both[:, t * LANES : (t + 1) * LANES]
 
-    base = twice(line)
-    base_mixed = twice(jnp.where(line < cut, SUB + line, line - cut))
-    base_odd = twice(medium_quads // 2 + line)
+    @jax.named_scope("start_table")
+    def start_table():
+        count = 2 * n
+        step = medium_quads * lax.broadcasted_iota(jnp.int32, (count, z.wrap), 0)
+        wave_cos[...], wave_sin[...] = turns(count, z.wrap, z.wrap, step)
 
     def wave(u):
         return wave_cos[pl.ds(u, 1), :], wave_sin[pl.ds(u, 1), :]
 
-    def fill_rows(i, _):
-        pair0, pair1 = [], []
-        for k in range(2):
-            p = 2 * i + k
+    @jax.named_scope("fill_table")
+    def fill_table(lo, hi):
+        base = twice(line_t)
+        mixed = twice(jnp.where(line_t < left_over, SUB + line_t, line_t - left_over))
+
+        def fill_rows(p, _):
             cos, sin = wave(2 * p)
-            pair0.append(turned(base, cos, sin))
+            upper = turned(base, cos, sin)
             low_cos, low_sin = wave(p)
-            cos = jnp.where(line < cut, cos, low_cos)
-            sin = jnp.where(line < cut, sin, low_sin)
-            pair1.append(turned(base_mixed, cos, sin))
-        at = pl.multiple_of(2 * SUB * i, 2 * SUB)
-        keep_rows(pl.ds(at, 2 * SUB), *pair0)
-        keep_rows(pl.ds(at + n * SUB, 2 * SUB), *pair1)
-        return 0
-
-    lax.fori_loop(0, n // 2, fill_rows, 0)
-
-    def fill_coarse(i, _):
-        cos, sin = wave(i)
-        at = pl.multiple_of(2 * SUB * (i + n), 2 * SUB)
-        keep_rows(pl.ds(at, 2 * SUB), turned(base, cos, sin), turned(base_odd, cos, sin))
-        return 0
-
-    lax.fori_loop(0, lat // 2, fill_coarse, 0)
-
-    def came_rows(i, _):
-        p = (me + i) % n
-        for t in range(2):
-            pltpu.make_async_remote_copy(
-                send.at[t, p], got.at[t, p], sent.at[t, p], came.at[t, p],
-                device_id=place(p), device_id_type=MESH,
-            ).wait()
-        return 0
-
-    lax.fori_loop(1, n, came_rows, 0)
-
-    def came_second(i, _):
-        p = (a + i) % lat
-        pltpu.make_async_remote_copy(
-            second.at[p], got_coarse.at[p], sent_two.at[p], came_two.at[p],
-            device_id={"scale": s, "lat": p}, device_id_type=MESH,
-        ).wait()
-        first_copy(p).wait_send()
-
-        @pl.when(p < far)
-        def _():
-            far_copy(p).wait_send()
-
-        return 0
-
-    lax.fori_loop(1, lat, came_second, 0)
+            cos = jnp.where(line_t < left_over, cos, low_cos)
+            sin = jnp.where(line_t < left_over, sin, low_sin)
+            at = pl.multiple_of(2 * SUB * p, 2 * SUB)
+            keep_rows(pl.ds(at, 2 * SUB), upper, turned(mixed, cos, sin))
+            return 0
+
+        lax.fori_loop(lo, hi, fill_rows, 0)
+
+    @jax.named_scope("end_table")
+    def end_table():
+        upper, lower = twice(4 * line_t), twice(4 * (SUB + line_t))
+        for u in range(4):
+            cos, sin = turns(1, z.wrap, z.wrap, u)
+            at = 2 * SUB * (n + u)
+            keep_rows(slice(at, at + 2 * SUB), turned(upper, cos, sin), turned(lower, cos, sin))
+
+    @jax.named_scope("collect")
+    def collect():
+        row_copy(0, n - 1).wait()
+        second_copy(0, lat - 1).wait()
+
+    @jax.named_scope("meet")
+    def meet():
+        pl.semaphore_wait(barrier, n - 1)
+
+    start(coarse_loads())
+    start(fine_loads(0))
+    start_table()
+    start(fine_loads(1))
+    fill_table(0, n // 2)
+    start(fine_loads(2))
+    fill_table(n // 2, n)
+    end_table()
+    start(fine_loads(3))
+    advance_coarse()
+    lax.fori_loop(0, 1, fine_group, 0)
+    start(medium_loads())
+    meet()
+    send_first()
+    lax.fori_loop(1, 2, fine_group, 0)
+    start(fine_loads(z.groups - 1))
+    lax.fori_loop(2, z.groups - 1, fine_group, 0)
+    put_fine(0, z.groups - 1)
+    medium_rows()
+    lax.fori_loop(z.groups - 1, z.groups, fine_group, 0)
+    put_fine(z.groups - 1, z.groups)
+    ship()
+    wait_first()
+    coarse_rows()
+    collect()
 
 
 def grid_kernel(
@@ -697,8 +671,10 @@
     for copy in copies:
         copy.start()
     many = 2 * z.n * SUB
+    fours = z.lat // 4
     turned[:, :many] = got[...].reshape(many, LANES).astype(jnp.float32).T.astype(jnp.bfloat16)
-    few = got_coarse[...].reshape(z.lat * SUB, LANES).astype(jnp.float32)
+    few = got_coarse[...].astype(jnp.float32).reshape(fours, 4, 2 * SUB, LANES)
+    few = (few[:, 0] + few[:, 1] + few[:, 2] + few[:, 3]).reshape(fours * 2 * SUB, LANES)
     turned[:, many:] = few.T.astype(jnp.bfloat16)
     e, tiles = z.members, z.wrap // LANES
     for t in range(tiles):
@@ -743,9 +719,11 @@
     f32, bf16, dma = jnp.float32, jnp.bfloat16, pltpu.SemaphoreType.DMA
     e, n, lat, rows = z.members, z.n, z.lat, z.rows
     tiles = z.medium_slots // LANES
-    far = -(-(z.coarse_slots - LANES) // z.piece)
-    table_rows = (2 * n + lat) * SUB
+    shared = z.piece - LANES // lat
+    table_rows = (n + lat // 4) * 2 * SUB
     operands = (
+        decay,
+        amplitude,
         fine_state.reshape(z.pairs, z.fine, z.fine_slots),
         fine_noise.reshape(z.pairs, z.fine, z.fine_slots),
         fine_basis,
@@ -759,19 +737,18 @@
     operands = tuple(pltpu.with_memory_space_constraint(x, pltpu.HBM) for x in operands)
     vmem = pl.BlockSpec(memory_space=pltpu.VMEM)
     hbm = pl.BlockSpec(memory_space=pltpu.HBM)
-    smem = pl.BlockSpec(memory_space=pltpu.SMEM)
     between = (
         pltpu.VMEM((z.pairs, z.fine, z.fine_slots), f32),
         pltpu.VMEM((tiles, e, z.medium, 2, LANES), f32),
         pltpu.VMEM((2, z.coarse, z.coarse_slots), f32),
-        pltpu.VMEM((2, n, SUB, LANES), bf16),
-        pltpu.VMEM((lat, SUB, LANES), bf16),
+        pltpu.VMEM((n, 2 * SUB, LANES), bf16),
+        pltpu.VMEM((lat, 2 * SUB, LANES), bf16),
         pltpu.VMEM((table_rows, 2 * z.wrap), bf16),
     )
     held = pl.pallas_call(
         functools.partial(spread_kernel, z),
         out_shape=between,
-        in_specs=[smem, smem] + [hbm] * 9,
+        in_specs=[hbm] * 11,
         out_specs=(vmem,) * 6,
         scratch_shapes=[
             pltpu.VMEM((z.groups, z.pairs, SUB, z.fine_slots), bf16),
@@ -782,36 +759,30 @@
             pltpu.VMEM((z.medium, rows, z.medium_slots), bf16),
             pltpu.VMEM((z.medium * z.pairs, z.medium_slots), bf16),
             pltpu.VMEM((rows * 3 * SUB, LANES), f32),
-            pltpu.VMEM((2, n, SUB, LANES), bf16),
+            pltpu.VMEM((n, 2 * SUB, LANES), bf16),
             pltpu.VMEM((2, z.coarse, z.coarse_slots), bf16),
             pltpu.VMEM((z.coarse, z.coarse_slots), bf16),
-            pltpu.VMEM((lat, 32, LANES), bf16),
-            pltpu.VMEM((far, 32, LANES), bf16),
+            pltpu.VMEM((32 * 3 * SUB, LANES), f32),
             pltpu.VMEM((lat, 32, LANES), bf16),
             pltpu.VMEM((lat, 32, LANES), bf16),
             pltpu.VMEM((lat * 5 * SUB, LANES), f32),
-            pltpu.VMEM((12 * lat, 2 * LANES), bf16),
-            pltpu.VMEM((12 * z.pairs, 2 * LANES), bf16),
-            pltpu.VMEM((lat * SUB, LANES), f32),
-            pltpu.VMEM((lat, SUB, LANES), bf16),
+            pltpu.VMEM(((z.piece + shared) * lat, LANES), bf16),
+            pltpu.VMEM((z.piece * z.pairs, LANES), bf16),
+            pltpu.VMEM((lat, 2 * SUB, LANES), bf16),
             pltpu.VMEM((2 * n, z.wrap), f32),
             pltpu.VMEM((2 * n, z.wrap), f32),
-            dma((3, z.groups)),
-            dma((2 * tiles + 1,)),
+            pltpu.SMEM((3,), f32),
+            pltpu.SMEM((3,), f32),
+            dma((z.groups,)),
+            dma,
+            dma,
             dma((3,)),
-            dma((2, n)),
-            dma((2, n)),
-            dma((lat,)),
-            dma((lat,)),
-            dma((lat,)),
-            dma((lat,)),
-            dma((lat,)),
-            dma((lat,)),
+            dma((3,)),
         ],
         compiler_params=pltpu.CompilerParams(
             collective_id=0, has_side_effects=True, vmem_limit_bytes=32 * 1024 * 1024
         ),
-    )(decay, amplitude, *operands)
+    )(*operands)
     fine_next, medium_next, coarse_next, pattern = pl.pallas_call(
         functools.partial(grid_kernel, z),
         out_shape=(

time: 32.2 us -> 24.1 us (0.75)
  Pallas kernels: 30.1 us -> 23.4 us
  local copies, waits for them, and re-layouts: 1.3 us -> 0 us
    pallas_call x1, Pallas kernels: 25.8 us -> 19.1 us  [fast_body(): pl.pallas_call(functools.partial(spread_kernel, z), out_shape=between, in...]
    unnamed x4 -> x0, local copies, waits for them, and re-layouts: 1.3 us -> none
where the time goes in v2:
time: 24.1 us; the launch traced here: 24 us
  Pallas kernels  23.4 us (97%)
  between operations  0.64 us (3%)
    pallas_call x1, Pallas kernels, fast_body(): pl.pallas_call(functools.partial(spread_kernel, z), out_shape=between, in...  19.1 us
    pallas_call x1, Pallas kernels, fast_body(): pl.pallas_call(functools.partial(grid_kernel, z), out_shape=(jax.ShapeDty...  4.3 us

profile of v2, /device:TPU:0, one launch (start us, length us, event | category | flops | bytes accessed | tf_op | source)
XLA Modules:
  0.0 24.0 jit_solution(14714492625025566824)
XLA Ops:
  0.6 19.1 %shard_map.138 = (f32[32,40,1280]{2,1,0:T(8,128)S(1)}, f32[5,16,20,2,128]{4,3,2,1,0:T(2,128)S(1)}, f32[2,160,160]{2,1,0:T(8,128)S(1)}, bf16[32,16,128]{2,1,0:T(8...) custom-call(f32[3]{0:T(128)} %decay_in.1, f32[3]{0:T(128)} %amp_in.1, ...), custom_call_target="tpu_custom_call" | custom-call | tf_op jit(solution)/shard_map/pallas_call | solution.py:748
  19.7 4.3 %shard_map.139 = (f32[32,40,1280]{2,1,0:T(8,128)}, f32[16,20,2,640]{3,2,1,0:T(2,128)}, f32[1,2,160,160]{3,2,1,0:T(8,128)}, f32[320,128]{1,0:T(8,128)}) custom-call(f32[32,40,1280]{2,1,0:T(8,128)S(1)} %get-tuple-element.14.fine_in, f32[5,16,20,2,128]{4,3,2,1,0:T(2,128)S(1)} %get-tuple-element.15.medium_in, f32[2,160,160]{2,1,0:T(8,128)S(1)} %get-tuple-element.16.coarse_in, ...), custom_call_target="tpu_custom_call" | custom-call | tf_op jit(solution)/shard_map/pallas_call | solution.py:786

commit v3 on v2

--- a/solution.py
+++ b/solution.py
@@ -227,7 +227,11 @@
         self.held, self.own, self.rows = coarse_state.shape[0], coarse_basis.shape[0], fine_basis.shape[1]
         self.groups = self.fine // SUB
         self.quad = LANES // self.pairs
-        self.piece = self.coarse // lat
+        self.medium_room = self.medium + 1
+        self.quarter, self.owners = lat // 4, lat // 2
+        self.piece = self.coarse // max(self.owners, 1)
+        self.low = LANES // max(self.owners, 1)
+        self.first_rows = -(-3 * self.low // SUB) * SUB
         self.wrap = NLON // max(self.quad, 1)
 
     def fits(self):
@@ -237,12 +241,14 @@
             return False
         if self.fine % SUB or self.medium % 4 or self.fine != 2 * self.medium:
             return False
-        if self.fine_slots % LANES or self.medium_slots % LANES or self.coarse % self.lat:
+        if self.fine_slots % (2 * LANES) or self.medium_slots % LANES or self.scale != 2:
             return False
         over = self.coarse_slots - LANES
-        if self.coarse_slots != self.coarse or over <= 0 or 2 * over > LANES or over % self.lat:
+        if self.coarse_slots != self.coarse or 4 * over != LANES or over % self.owners:
             return False
-        if 3 * self.piece > 32 or self.lat % 4 or LANES * self.pairs // self.lat % LANES:
+        if self.owners != SUB or self.coarse % self.owners or over // self.owners != 4 or self.low % 4 or self.piece > 4 * SUB:
+            return False
+        if self.n * self.fine > self.fine_slots or self.n * self.medium > self.medium_slots:
             return False
         high = self.fine // 4
         return SUB <= high and high - SUB + self.medium // 4 <= SUB and self.wrap % LANES == 0
@@ -280,6 +286,7 @@
     noise_m,
     basis_m,
     half_m,
+    picked_m,
     rows_f,
     send,
     noise_c,
@@ -300,6 +307,7 @@
     load_c,
     sent,
     came,
+    twin,
 ):
     n, lat = z.n, z.lat
     s, a = lax.axis_index("scale"), lax.axis_index("lat")
@@ -315,11 +323,15 @@
 
     barrier = pltpu.get_barrier_semaphore()
 
-    def greet(i, _):
-        pl.semaphore_signal(barrier, inc=1, device_id=place((me + i) % n), device_id_type=MESH)
-        return 0
-
-    lax.fori_loop(1, n, greet, 0)
+    quarter, owners = z.quarter, z.owners
+    owner = (a >= quarter) & (a < quarter + owners)
+    mine = jnp.where(owner, a - quarter, 0)
+
+    def greet():
+        for i in range(1, lat):
+            near = {"scale": s, "lat": (a + i) % lat}
+            pl.semaphore_signal(barrier, inc=1, device_id=near, device_id_type=MESH)
+        pl.semaphore_signal(barrier, inc=1, device_id={"scale": 1 - s, "lat": a}, device_id_type=MESH)
 
     def coarse_loads():
         return (
@@ -330,25 +342,43 @@
             pltpu.make_async_copy(coarse_basis.at[0], basis_c, load_c),
         )
 
-    def fine_loads(g):
-        rows = pl.ds(pl.multiple_of(g * SUB, SUB), SUB)
-        return (
-            pltpu.make_async_copy(fine_state.at[:, rows, :], fine_next.at[:, rows, :], load_f.at[g]),
-            pltpu.make_async_copy(fine_noise.at[:, rows, :], noise_f.at[g], load_f.at[g]),
-            pltpu.make_async_copy(fine_basis.at[rows], basis_f.at[rows], load_f.at[g]),
-        )
-
-    def medium_loads():
-        copies = [pltpu.make_async_copy(medium_basis, basis_m, load_m)]
-        for t in range(mid_tiles):
-            cols = pl.ds(t * LANES, LANES)
+    wide = 2 * LANES
+    chunks = z.fine_slots // wide
+    fine_limit = z.fine_slots - me * z.fine
+    medium_limit = z.medium_slots - me * z.medium
+
+    def fine_loads(k):
+        cols = pl.ds(k * wide if isinstance(k, int) else pl.multiple_of(k * wide, wide), wide)
+        copies = [
+            pltpu.make_async_copy(fine_state.at[:, :, cols], fine_next.at[:, :, cols], load_f.at[k]),
+            pltpu.make_async_copy(fine_basis.at[:, :, cols], basis_f.at[:, :, cols], load_f.at[k]),
+        ]
+        for g in range(z.groups):
+            rows = pl.ds(g * SUB, SUB)
             copies.append(
-                pltpu.make_async_copy(medium_state.at[:, :, :, cols], medium_next.at[t], load_m)
-            )
-            copies.append(
-                pltpu.make_async_copy(medium_noise.at[:, :, :, cols], noise_m.at[t], load_m)
+                pltpu.make_async_copy(fine_noise.at[:, rows, cols], noise_f.at[g, :, :, cols], load_f.at[k])
             )
         return copies
+
+    def medium_loads(t):
+        cols = pl.ds(t * LANES if isinstance(t, int) else pl.multiple_of(t * LANES, LANES), LANES)
+        return (
+            pltpu.make_async_copy(
+                medium_state.at[:, :, :, cols], medium_next.at[t, :, pl.ds(0, z.medium)], load_m.at[t]
+            ),
+            pltpu.make_async_copy(medium_noise.at[:, :, :, cols], noise_m.at[t], load_m.at[t]),
+            pltpu.make_async_copy(medium_basis.at[:, :, cols], basis_m.at[t], load_m.at[t]),
+        )
+
+    def start_fine(k):
+        @pl.when(k * wide < fine_limit)
+        def _():
+            start(fine_loads(k))
+
+    def start_medium(t):
+        @pl.when(t * LANES < medium_limit)
+        def _():
+            start(medium_loads(t))
 
     def start(copies):
         for copy in copies:
@@ -369,69 +399,67 @@
             coarse_next[c] = new
             planes.append(new)
         planes.append(basis_c[...].astype(f32))
-        column_c = lax.broadcasted_iota(jnp.int32, (lat, LANES), 1)
+        column_c = lax.broadcasted_iota(jnp.int32, (over, LANES), 1)
         for k, plane in enumerate(planes):
             rest = plane[:over, LANES:]
-            rest = jnp.concatenate([jnp.zeros_like(rest), rest, jnp.zeros((over, LANES - 2 * over), f32)], axis=1)
-            for i in range(z.piece):
-                rows = plane[i * lat : (i + 1) * lat, :LANES]
-                low = i * lat - LANES
-                if low >= 0:
-                    rows = jnp.where(column_c < over, rows, rest[low : low + lat])
-                spread[pl.ds((3 * i + k) * pitch, lat), :] = rows
-        for p in range(lat):
-            first[p] = spread[pl.ds(p, 32, stride=pitch), :].astype(bf16)
-
-    def first_copy(p, count=None):
-        at = p if count is None else pl.ds(p, count)
-        to = a if count is None else at
+            last = plane[LANES:, : 2 * over]
+            added = jnp.concatenate([jnp.zeros_like(last), last[:, :over], rest], axis=1)
+            folded = jnp.where(column_c < 2 * over, plane[LANES - over : LANES, :LANES], added)
+            for i in range(z.low):
+                lo = i * owners - (LANES - over)
+                rows = folded[lo : lo + owners] if lo >= 0 else plane[i * owners : (i + 1) * owners, :LANES]
+                spread[(3 * i + k) * owners : (3 * i + k + 1) * owners, :] = rows
+        for o in range(owners):
+            first[o] = spread[pl.ds(o, z.first_rows, stride=owners), :].astype(bf16)
+
+    def all_of(ref, count, k):
+        some = ref.at[pl.ds(0, count)]
         return pltpu.make_async_remote_copy(
-            first.at[at], landed.at[to], sent.at[0], came.at[0],
+            some, some, sent.at[k], came.at[k], device_id={"scale": 1 - s, "lat": a}, device_id_type=MESH
+        )
+
+    def first_copy(o):
+        return pltpu.make_async_remote_copy(
+            first.at[o], landed.at[a], sent.at[0], came.at[0],
+            device_id={"scale": s, "lat": quarter + o}, device_id_type=MESH,
+        )
+
+    def second_copy(p):
+        return pltpu.make_async_remote_copy(
+            second.at[p], got_coarse.at[mine], sent.at[1], came.at[1],
             device_id={"scale": s, "lat": p}, device_id_type=MESH,
         )
 
-    def second_copy(p, count=None):
-        at = p if count is None else pl.ds(p, count)
-        to = a if count is None else at
+    def row_copy(p):
         return pltpu.make_async_remote_copy(
-            second.at[at], got_coarse.at[to], sent.at[1], came.at[1],
-            device_id={"scale": s, "lat": p}, device_id_type=MESH,
-        )
-
-    def row_copy(p, count=None):
-        at = p if count is None else pl.ds(p, count)
-        to = me if count is None else at
-        return pltpu.make_async_remote_copy(
-            send.at[at], got.at[to], sent.at[2], came.at[2],
+            send.at[p], got.at[me], sent.at[2], came.at[2],
             device_id=place(p), device_id_type=MESH,
         )
 
     lane = lax.broadcasted_iota(jnp.int32, (z.rows, 2 * LANES), 1) % SUB
-    shift = lax.broadcasted_iota(jnp.int32, (SUB, z.fine_slots), 0)
-    slack = z.fine_slots - me * z.fine - shift - lax.broadcasted_iota(jnp.int32, (SUB, z.fine_slots), 1)
-
-    @jax.named_scope("fine_group")
-    def fine_group(g, _):
-        for copy in fine_loads(g):
+    slack = fine_limit - lax.broadcasted_iota(jnp.int32, (SUB, wide), 0)
+    slack = slack - lax.broadcasted_iota(jnp.int32, (SUB, wide), 1)
+
+    @jax.named_scope("fine_chunk")
+    def fine_chunk(k, _):
+        for copy in fine_loads(k):
             copy.wait()
-        rows = pl.ds(pl.multiple_of(g * SUB, SUB), SUB)
-        keep = slack > g * SUB
-
-        def pair(i, _):
-            new = decay[0] * fine_next[pl.ds(2 * i, 2), rows, :] + amp[0] * noise_f[g, pl.ds(2 * i, 2)].astype(f32)
-            new = jnp.where(keep[None], new, 0.0)
-            fine_next[pl.ds(2 * i, 2), rows, :] = new
-            at = pl.ds(pl.multiple_of(2 * SUB * i, 2 * SUB), 2 * SUB)
-            half[at, :] = new.reshape(2 * SUB, z.fine_slots).astype(bf16)
-            return 0
-
-        lax.fori_loop(0, z.pairs // 2, pair, 0)
-        basis = basis_f[rows].reshape(SUB * z.rows, z.fine_slots)
-        all_pairs = lax.dot_general(basis, half[...], (((1,), (1,)), ((), ())), preferred_element_type=f32)
-        total = all_pairs[: z.rows]
-        for q in range(1, SUB):
-            total = jnp.where(lane == q, all_pairs[q * z.rows : (q + 1) * z.rows], total)
-        picked[pl.ds(pl.multiple_of(g * z.rows, z.rows), z.rows), :] = total.astype(bf16)
+        cols = pl.ds(pl.multiple_of(k * wide, wide), wide)
+        for g in range(z.groups):
+            rows = slice(g * SUB, (g + 1) * SUB)
+            keep = slack > g * SUB + k * wide
+            for i in range(z.pairs // 2):
+                two = slice(2 * i, 2 * i + 2)
+                new = decay[0] * fine_next[two, rows, cols] + amp[0] * noise_f[g, two, :, cols].astype(f32)
+                new = jnp.where(keep[None], new, 0.0)
+                fine_next[two, rows, cols] = new
+                half[g, 2 * SUB * i : 2 * SUB * (i + 1), :] = new.reshape(2 * SUB, wide).astype(bf16)
+            basis = basis_f[rows, :, cols].reshape(SUB * z.rows, wide)
+            all_pairs = lax.dot_general(basis, half[g], (((1,), (1,)), ((), ())), preferred_element_type=f32)
+            total = all_pairs[: z.rows]
+            for q in range(1, SUB):
+                total = jnp.where(lane == q, all_pairs[q * z.rows : (q + 1) * z.rows], total)
+            picked[g * z.rows : (g + 1) * z.rows, :] += total
         return 0
 
     target = lax.broadcasted_iota(jnp.int32, (2 * LANES, 2 * LANES), 1)
@@ -440,7 +468,7 @@
     order = (lax.broadcasted_iota(jnp.int32, (2 * LANES, 2 * LANES), 0) == wanted).astype(f32).astype(bf16)
     @jax.named_scope("put_fine")
     def put_fine(g0, g1):
-        moved = jnp.dot(picked[g0 * z.rows : g1 * z.rows, :], order, preferred_element_type=f32)
+        moved = jnp.dot(picked[g0 * z.rows : g1 * z.rows, :].astype(bf16), order, preferred_element_type=f32)
         for g in range(g0, g1):
             for q in range(2):
                 rows_f[pl.ds(2 * g + q, z.rows, stride=stride), :] = moved[
@@ -457,119 +485,142 @@
     @jax.named_scope("ship")
     def ship():
         scale_row = jnp.concatenate([weight(0, me), weight(fine_quads - SUB, me)], axis=0)
-
-        def cast(r, _):
-            at = pl.ds(pl.multiple_of(r * stride, SUB), 2 * SUB)
-            send[r] = (rows_f[at, :].astype(bf16).astype(f32) * scale_row).astype(bf16)
-            return 0
-
-        lax.fori_loop(0, z.rows, cast, 0, unroll=4)
-        for i in range(1, n):
-            row_copy((me + i) % n).start()
+        for r in range(z.rows):
+            rows = rows_f[r * stride : r * stride + 2 * SUB, :]
+            send[r] = (rows.astype(bf16).astype(f32) * scale_row).astype(bf16)
+        for i in range(1, lat):
+            row_copy(s * lat + (a + i) % lat).start()
+        pl.semaphore_wait(twin, 1)
+        for i in range(lat):
+            row_copy((1 - s) * lat + (a + i) % lat).start()
         got[me] = send[me]
 
     @jax.named_scope("send_first")
     def send_first():
-        for i in range(1, lat):
-            first_copy((a + i) % lat).start()
-        landed[a] = first[a]
-
-    @jax.named_scope("medium_rows")
-    def medium_rows():
-        for copy in medium_loads():
+        for i in range(owners):
+            o = (a + i) % owners
+
+            @pl.when(o + quarter != a)
+            def _():
+                first_copy(o).start()
+
+        @pl.when(owner)
+        def _():
+            landed[a] = first[mine]
+
+    flat_next = medium_next.reshape(mid_tiles * z.pairs * z.medium_room, LANES)
+    flat_noise = noise_m.reshape(mid_tiles * z.pairs * z.medium, LANES)
+    span, leap = 2 * z.medium, 2 * z.medium_room
+    room = medium_limit - lax.broadcasted_iota(jnp.int32, (span, LANES), 0) // 2
+    room = room - lax.broadcasted_iota(jnp.int32, (span, LANES), 1)
+    lane4 = lax.broadcasted_iota(jnp.int32, (z.rows, LANES), 1) // z.pairs
+
+    @jax.named_scope("medium_chunk")
+    def medium_chunk(t, _):
+        for copy in medium_loads(t):
             copy.wait()
-        flat_next = medium_next.reshape(mid_tiles * z.pairs * z.medium, LANES)
-        flat_noise = noise_m.reshape(mid_tiles * z.pairs * z.medium, LANES)
-        span = 2 * z.medium
-        room = z.medium_slots - me * z.medium - lax.broadcasted_iota(jnp.int32, (span, LANES), 0) // 2
-        room = room - lax.broadcasted_iota(jnp.int32, (span, LANES), 1)
-
-        def medium_member(e, _):
-            for t in range(mid_tiles):
-                at = pl.ds(pl.multiple_of((t * z.members + e) * span, SUB), span)
-                new = decay[1] * flat_next[at, :] + amp[1] * flat_noise[at, :].astype(f32)
-                flat_next[at, :] = jnp.where(room > t * LANES, new, 0.0)
-            return 0
-
-        lax.fori_loop(0, z.members, medium_member, 0)
-
-        def medium_mode(m, _):
-            for c in range(2):
-                at = pl.ds(pl.multiple_of(m * z.pairs + c * z.members, z.members), z.members)
-                for t in range(mid_tiles):
-                    new = flat_next[pl.ds(t * z.members * span + 2 * m + c, z.members, stride=span), :]
-                    half_m[at, t * LANES : (t + 1) * LANES] = new.astype(bf16)
-            return 0
-
-        lax.fori_loop(0, z.medium, medium_mode, 0)
-        lane4 = lax.broadcasted_iota(jnp.int32, (z.rows, LANES), 1) // z.pairs
+        keep = room > t * LANES
+        top = t * z.members * leap
+        for e in range(z.members):
+            at = pl.ds(pl.multiple_of(top + e * leap, 2), span)
+            noise_at = pl.ds(pl.multiple_of((t * z.members + e) * span, SUB), span)
+            new = decay[1] * flat_next[at, :] + amp[1] * flat_noise[noise_at, :].astype(f32)
+            flat_next[at, :] = jnp.where(keep, new, 0.0)
         for q in range(medium_quads):
-            basis = basis_m[4 * q : 4 * q + 4].reshape(4 * z.rows, z.medium_slots)
+            for b in range(4):
+                for c in range(2):
+                    new = flat_next[pl.ds(top + 2 * (4 * q + b) + c, z.members, stride=leap), :]
+                    at = q * LANES + b * z.pairs + c * z.members
+                    half_m[at : at + z.members, :] = new.astype(bf16)
+            basis = basis_m[t, 4 * q : 4 * q + 4].reshape(4 * z.rows, LANES)
             all_pairs = lax.dot_general(
                 basis, half_m[q * LANES : (q + 1) * LANES, :], (((1,), (1,)), ((), ())), preferred_element_type=f32
             )
             total = all_pairs[: z.rows]
             for b in range(1, 4):
                 total = jnp.where(lane4 == b, all_pairs[b * z.rows : (b + 1) * z.rows], total)
-            rows_f[pl.ds(fine_quads + q, z.rows, stride=stride), :] = total
+            picked_m[q * z.rows : (q + 1) * z.rows, :] += total
+        return 0
+
+    @jax.named_scope("put_medium")
+    def put_medium():
+        for q in range(medium_quads):
+            rows_f[pl.ds(fine_quads + q, z.rows, stride=stride), :] = picked_m[q * z.rows : (q + 1) * z.rows, :]
         for spare in range(fine_quads + medium_quads, 2 * SUB):
             rows_f[pl.ds(spare, z.rows, stride=stride), :] = jnp.zeros((z.rows, LANES), f32)
 
+    @jax.named_scope("fill_zeros")
+    def fill_zeros():
+        def fine_fill(k, _):
+            cols = pl.ds(pl.multiple_of(k * wide, wide), wide)
+
+            def pair_fill(i, _):
+                fine_next[pl.ds(2 * i, 2), :, cols] = jnp.zeros((2, z.fine, wide), f32)
+                return 0
+
+            return lax.fori_loop(0, z.pairs // 2, pair_fill, 0)
+
+        lax.fori_loop((fine_limit + wide - 1) // wide, chunks, fine_fill, 0)
+
+        def medium_fill(t, _):
+            def member_fill(e, _):
+                at = pl.ds(pl.multiple_of((t * z.members + e) * leap, 2), span)
+                flat_next[at, :] = jnp.zeros((span, LANES), f32)
+                return 0
+
+            return lax.fori_loop(0, z.members, member_fill, 0)
+
+        lax.fori_loop((medium_limit + LANES - 1) // LANES, mid_tiles, medium_fill, 0)
+
     @jax.named_scope("wait_first")
     def wait_first():
-        first_copy(0, lat - 1).wait()
+        all_of(landed, lat - 1, 0).wait_recv()
 
     @jax.named_scope("coarse_rows")
     def coarse_rows():
-        jump = 5 * SUB
-
-        def widen(p, _):
-            landed_f[pl.ds(pl.multiple_of(p * jump, SUB), 32), :] = landed[p].astype(f32)
-            return 0
-
-        lax.fori_loop(0, lat, widen, 0, unroll=4)
+        jump = z.first_rows + SUB
+        for p in range(lat):
+            landed_f[p * jump : p * jump + z.first_rows, :] = landed[p].astype(f32)
         lane = lax.broadcasted_iota(jnp.int32, (lat, LANES), 1)
-        shared = LANES // lat
-        for i in range(z.piece):
+        low, extra = z.low, over // owners
+        plain = low - extra
+        for i in range(low):
             for c in range(2):
                 values = landed_f[pl.ds(3 * i + c, lat, stride=jump), :]
                 right_c[i * z.pairs + c * z.members : i * z.pairs + (c + 1) * z.members, :] = values.astype(bf16)
             values = landed_f[pl.ds(3 * i + 2, lat, stride=jump), :]
-            if i >= shared:
-                extra = jnp.where(lane >= over, values, 0.0)
-                values = jnp.where(lane < over, values, 0.0)
-                left_c[(z.piece + i - shared) * lat : (z.piece + i - shared + 1) * lat, :] = extra.astype(bf16)
-            left_c[i * lat : (i + 1) * lat, :] = values.astype(bf16)
+            if i >= plain:
+                j = i - plain
+                for at, lo, hi in ((i, 0, 2), (i + extra, 2, 3), (z.piece + j, 3, 4)):
+                    some = jnp.where((lane >= lo * over) & (lane < hi * over), values, 0.0)
+                    left_c[at * lat : (at + 1) * lat, :] = some.astype(bf16)
+            else:
+                left_c[i * lat : (i + 1) * lat, :] = values.astype(bf16)
         all_pairs = lax.dot_general(
             left_c[...], right_c[...], (((1,), (1,)), ((), ())), preferred_element_type=f32
         )
-        slot = lax.broadcasted_iota(jnp.int32, (lat, z.piece * z.pairs), 1) // z.pairs
-        total = all_pairs[:lat]
-        for i in range(1, z.piece):
-            total = jnp.where(slot == i, all_pairs[i * lat : (i + 1) * lat], total)
-        extra = all_pairs[z.piece * lat : (z.piece + 1) * lat]
-        for i in range(shared + 1, z.piece):
-            extra = jnp.where(slot == i, all_pairs[(z.piece + i - shared) * lat : (z.piece + i - shared + 1) * lat], extra)
         block = lane // z.pairs
-        for i in range(z.piece):
-            j = i // 4
-            row = total[:, j * LANES : min((j + 1) * LANES, total.shape[1])]
-            if i < z.piece - shared:
-                far = extra[:, shared * z.pairs + j * LANES :]
-                row = row + jnp.concatenate([far, jnp.zeros((lat, LANES - far.shape[1]), f32)], axis=1)
-            if row.shape[1] < LANES:
-                row = jnp.concatenate([row, jnp.zeros((lat, LANES - row.shape[1]), f32)], axis=1)
-            row = pltpu.roll(row, ((a % 4 - i % 4 + 4) % 4) * z.pairs, axis=1)
-            spread[pl.ds(i, lat, stride=pitch), :] = jnp.where(block == a % 4, row, 0.0)
-        for i in range(z.piece, 2 * SUB):
-            spread[pl.ds(i, lat, stride=pitch), :] = jnp.zeros((lat, LANES), f32)
-        scale_row = jnp.concatenate([weight(0, a), jnp.ones((SUB, LANES), f32)], axis=0)
+
+        def tile(i, j):
+            return all_pairs[i * lat : (i + 1) * lat, j * LANES : (j + 1) * LANES]
+
+        for j in range(SUB):
+            row = jnp.zeros((lat, LANES), f32)
+            for t in range(4):
+                i = 4 * j + t
+                if i < z.piece:
+                    value = tile(i, min(i, low - 1) // 4)
+                    if i < extra:
+                        value = value + tile(z.piece + i, (low - 1) // 4)
+                    row = jnp.where(block == t, value, row)
+            spread[pl.ds(j, lat, stride=pitch), :] = row
+        scale_row = weight(0, mine)
         for p in range(lat):
-            rows = spread[p * pitch : p * pitch + 2 * SUB, :].astype(bf16).astype(f32)
+            rows = spread[p * pitch : p * pitch + SUB, :].astype(bf16).astype(f32)
             second[p] = (rows * scale_row).astype(bf16)
         for i in range(1, lat):
             second_copy((a + i) % lat).start()
-        got_coarse[a] = second[a]
+        got_coarse[mine] = second[a]
 
     line_t = lax.broadcasted_iota(jnp.int32, (SUB, z.wrap), 0)
     left_over = fine_quads - SUB
@@ -612,49 +663,86 @@
             keep_rows(pl.ds(at, 2 * SUB), upper, turned(mixed, cos, sin))
             return 0
 
-        lax.fori_loop(lo, hi, fill_rows, 0)
+        lax.fori_loop(lo, hi, fill_rows, 0, unroll=2)
 
     @jax.named_scope("end_table")
     def end_table():
-        upper, lower = twice(4 * line_t), twice(4 * (SUB + line_t))
-        for u in range(4):
-            cos, sin = turns(1, z.wrap, z.wrap, u)
-            at = 2 * SUB * (n + u)
-            keep_rows(slice(at, at + 2 * SUB), turned(upper, cos, sin), turned(lower, cos, sin))
+        base = twice(owners * line_t)
+        at = 2 * SUB * n
+        tiles = []
+        for u in range(owners // 4):
+            for t in range(4):
+                cos, sin = turns(1, z.wrap, z.wrap, u + owners // 4 * t)
+                tiles.append(turned(base, cos, sin))
+        for q in range(0, len(tiles), 2):
+            keep_rows(slice(at + q * SUB, at + (q + 2) * SUB), tiles[q], tiles[q + 1])
 
     @jax.named_scope("collect")
     def collect():
-        row_copy(0, n - 1).wait()
-        second_copy(0, lat - 1).wait()
+        with jax.named_scope("rows_in"):
+            all_of(got, n - 1, 2).wait()
+
+        @pl.when(owner)
+        def _():
+            all_of(first, owners - 1, 0).wait_send()
+            all_of(second, lat - 1, 1).wait_send()
+            all_of(got_coarse, owners - 1, 1).wait_recv()
+
+        @pl.when(jnp.logical_not(owner))
+        def _():
+            all_of(first, owners, 0).wait_send()
+            all_of(got_coarse, owners, 1).wait_recv()
 
     @jax.named_scope("meet")
     def meet():
-        pl.semaphore_wait(barrier, n - 1)
-
+        pl.semaphore_wait(barrier, lat)
+        pl.semaphore_signal(twin, inc=1, device_id={"scale": 1 - s, "lat": a}, device_id_type=MESH)
+
+    fine_count = (fine_limit + wide - 1) // wide
+    half_way = jnp.minimum(fine_count, 3)
+    early = jnp.where(me < 2, half_way, jnp.where(me < SUB, 1, 0))
+    many = fine_count > 3
     start(coarse_loads())
-    start(fine_loads(0))
+    greet()
+
+    @pl.when(many)
+    def _():
+        start(fine_loads(0))
+
     start_table()
-    start(fine_loads(1))
-    fill_table(0, n // 2)
-    start(fine_loads(2))
-    fill_table(n // 2, n)
-    end_table()
-    start(fine_loads(3))
+
+    @pl.when(jnp.logical_not(many))
+    def _():
+        start(fine_loads(0))
+
+    start_fine(1)
+    picked[...] = jnp.zeros_like(picked)
+    picked_m[...] = jnp.zeros_like(picked_m)
     advance_coarse()
-    lax.fori_loop(0, 1, fine_group, 0)
-    start(medium_loads())
+    start_fine(2)
+    for t in range(mid_tiles):
+        start_medium(t)
+    for k in range(3, chunks):
+        start_fine(k)
+    lax.fori_loop(0, early, fine_chunk, 0)
     meet()
     send_first()
-    lax.fori_loop(1, 2, fine_group, 0)
-    start(fine_loads(z.groups - 1))
-    lax.fori_loop(2, z.groups - 1, fine_group, 0)
-    put_fine(0, z.groups - 1)
-    medium_rows()
-    lax.fori_loop(z.groups - 1, z.groups, fine_group, 0)
-    put_fine(z.groups - 1, z.groups)
+    lax.fori_loop(early, half_way, fine_chunk, 0)
+    lax.fori_loop(0, (medium_limit + LANES - 1) // LANES, medium_chunk, 0)
+    lax.fori_loop(half_way, fine_count, fine_chunk, 0)
+    put_fine(0, z.groups)
+    put_medium()
+
     ship()
-    wait_first()
-    coarse_rows()
+
+    @pl.when(owner)
+    def _():
+        wait_first()
+        coarse_rows()
+
+    fill_table(0, n)
+    end_table()
+    fill_zeros()
     collect()
 
 
@@ -667,15 +755,37 @@
     ]
     for t in range(medium_in.shape[0]):
         cols = pl.ds(t * LANES, LANES)
-        copies.append(pltpu.make_async_copy(medium_in.at[t], medium_out.at[:, :, :, cols], sems.at[2 + t]))
+        copies.append(pltpu.make_async_copy(medium_in.at[t, :, pl.ds(0, z.medium)], medium_out.at[:, :, :, cols], sems.at[2 + t]))
     for copy in copies:
         copy.start()
+    with jax.named_scope("turn_rows"):
+        turn_rows(z, got, got_coarse, turned)
+    with jax.named_scope("sum_longitudes"):
+        sum_longitudes(z, turned, table, out)
+    with jax.named_scope("wait_writes"):
+        for copy in copies:
+            copy.wait()
+
+
+def turn_rows(z, got, got_coarse, turned):
     many = 2 * z.n * SUB
-    fours = z.lat // 4
     turned[:, :many] = got[...].reshape(many, LANES).astype(jnp.float32).T.astype(jnp.bfloat16)
-    few = got_coarse[...].astype(jnp.float32).reshape(fours, 4, 2 * SUB, LANES)
-    few = (few[:, 0] + few[:, 1] + few[:, 2] + few[:, 3]).reshape(fours * 2 * SUB, LANES)
+    block = lax.broadcasted_iota(jnp.int32, (SUB, LANES), 1) // z.pairs
+    few = []
+    for u in range(z.owners // 4):
+        for t in range(4):
+            rows = jnp.zeros((SUB, LANES), jnp.float32)
+            for b in range(4):
+                some = got_coarse[4 * u + b].astype(jnp.float32)
+                if b != t:
+                    some = pltpu.roll(some, (b - t) % 4 * z.pairs, axis=1)
+                rows = jnp.where(block == b, some, rows)
+            few.append(rows)
+    few = jnp.concatenate(few, axis=0)
     turned[:, many:] = few.T.astype(jnp.bfloat16)
+
+
+def sum_longitudes(z, turned, table, out):
     e, tiles = z.members, z.wrap // LANES
     for t in range(tiles):
         both = jnp.dot(turned[...], table[:, 2 * t * LANES : 2 * (t + 1) * LANES], preferred_element_type=jnp.float32)
@@ -698,8 +808,6 @@
                 term = (re, -im, -re, im)[b * h % 4]
                 total = term if total is None else total + term
             out[pl.ds(h * tiles + t, e, stride=4 * tiles), :] = jnp.tanh(total)
-    for copy in copies:
-        copy.wait()
 
 
 def fast_body(
@@ -719,8 +827,8 @@
     f32, bf16, dma = jnp.float32, jnp.bfloat16, pltpu.SemaphoreType.DMA
     e, n, lat, rows = z.members, z.n, z.lat, z.rows
     tiles = z.medium_slots // LANES
-    shared = z.piece - LANES // lat
-    table_rows = (n + lat // 4) * 2 * SUB
+    owners = z.owners
+    table_rows = 2 * n * SUB + owners * SUB
     operands = (
         decay,
         amplitude,
@@ -739,10 +847,10 @@
     hbm = pl.BlockSpec(memory_space=pltpu.HBM)
     between = (
         pltpu.VMEM((z.pairs, z.fine, z.fine_slots), f32),
-        pltpu.VMEM((tiles, e, z.medium, 2, LANES), f32),
+        pltpu.VMEM((tiles, e, z.medium_room, 2, LANES), f32),
         pltpu.VMEM((2, z.coarse, z.coarse_slots), f32),
         pltpu.VMEM((n, 2 * SUB, LANES), bf16),
-        pltpu.VMEM((lat, 2 * SUB, LANES), bf16),
+        pltpu.VMEM((owners, SUB, LANES), bf16),
         pltpu.VMEM((table_rows, 2 * z.wrap), bf16),
     )
     held = pl.pallas_call(
@@ -753,31 +861,33 @@
         scratch_shapes=[
             pltpu.VMEM((z.groups, z.pairs, SUB, z.fine_slots), bf16),
             pltpu.VMEM((z.fine, rows, z.fine_slots), bf16),
-            pltpu.VMEM((SUB * z.pairs, z.fine_slots), bf16),
-            pltpu.VMEM((z.groups * rows, 2 * LANES), bf16),
+            pltpu.VMEM((z.groups, SUB * z.pairs, 2 * LANES), bf16),
+            pltpu.VMEM((z.groups * rows, 2 * LANES), f32),
             pltpu.VMEM((tiles, e, z.medium, 2, LANES), bf16),
-            pltpu.VMEM((z.medium, rows, z.medium_slots), bf16),
-            pltpu.VMEM((z.medium * z.pairs, z.medium_slots), bf16),
+            pltpu.VMEM((tiles, z.medium, rows, LANES), bf16),
+            pltpu.VMEM((z.medium * z.pairs, LANES), bf16),
+            pltpu.VMEM((z.medium // 4 * rows, LANES), f32),
             pltpu.VMEM((rows * 3 * SUB, LANES), f32),
             pltpu.VMEM((n, 2 * SUB, LANES), bf16),
             pltpu.VMEM((2, z.coarse, z.coarse_slots), bf16),
             pltpu.VMEM((z.coarse, z.coarse_slots), bf16),
-            pltpu.VMEM((32 * 3 * SUB, LANES), f32),
-            pltpu.VMEM((lat, 32, LANES), bf16),
-            pltpu.VMEM((lat, 32, LANES), bf16),
-            pltpu.VMEM((lat * 5 * SUB, LANES), f32),
-            pltpu.VMEM(((z.piece + shared) * lat, LANES), bf16),
-            pltpu.VMEM((z.piece * z.pairs, LANES), bf16),
-            pltpu.VMEM((lat, 2 * SUB, LANES), bf16),
+            pltpu.VMEM((max(z.first_rows * owners, lat * 3 * SUB), LANES), f32),
+            pltpu.VMEM((owners, z.first_rows, LANES), bf16),
+            pltpu.VMEM((lat, z.first_rows, LANES), bf16),
+            pltpu.VMEM((lat * (z.first_rows + SUB), LANES), f32),
+            pltpu.VMEM(((2 * z.piece - z.low) * lat, LANES), bf16),
+            pltpu.VMEM((z.low * z.pairs, LANES), bf16),
+            pltpu.VMEM((lat, SUB, LANES), bf16),
             pltpu.VMEM((2 * n, z.wrap), f32),
             pltpu.VMEM((2 * n, z.wrap), f32),
             pltpu.SMEM((3,), f32),
             pltpu.SMEM((3,), f32),
-            dma((z.groups,)),
-            dma,
+            dma((z.fine_slots // (2 * LANES),)),
+            dma((tiles,)),
             dma,
             dma((3,)),
             dma((3,)),
+            pltpu.SemaphoreType.REGULAR,
         ],
         compiler_params=pltpu.CompilerParams(
             collective_id=0, has_side_effects=True, vmem_limit_bytes=32 * 1024 * 1024

time: 24.1 us -> 20.2 us (0.84)
  Pallas kernels: 23.4 us -> 19.4 us
    pallas_call x1, Pallas kernels: 19.1 us -> 15.3 us  [fast_body(): pl.pallas_call(functools.partial(spread_kernel, z), out_shape=between, in...]
where the time goes in v3:
time: 20.2 us; the launch traced here: 20.1 us
  Pallas kernels  19.4 us (96%)
  between operations  0.64 us (3%)
    pallas_call x1, Pallas kernels, fast_body(): pl.pallas_call(functools.partial(spread_kernel, z), out_shape=between, in...  15.3 us
    pallas_call x1, Pallas kernels, fast_body(): pl.pallas_call(functools.partial(grid_kernel, z), out_shape=(jax.ShapeDty...  4.1 us

profile of v3, /device:TPU:0, one launch (start us, length us, event | category | flops | bytes accessed | tf_op | source)
XLA Modules:
  0.0 20.1 jit_solution(3304272579261337434)
XLA Ops:
  0.6 15.3 %shard_map.138 = (f32[32,40,1280]{2,1,0:T(8,128)S(1)}, f32[5,16,21,2,128]{4,3,2,1,0:T(2,128)S(1)}, f32[2,160,160]{2,1,0:T(8,128)S(1)}, bf16[32,16,128]{2,1,0:T(8...) custom-call(f32[3]{0:T(128)} %decay_in.1, f32[3]{0:T(128)} %amp_in.1, ...), custom_call_target="tpu_custom_call" | custom-call | tf_op jit(solution)/shard_map/pallas_call | solution.py:856
  15.9 4.1 %shard_map.139 = (f32[32,40,1280]{2,1,0:T(8,128)}, f32[16,20,2,640]{3,2,1,0:T(2,128)}, f32[1,2,160,160]{3,2,1,0:T(8,128)}, f32[320,128]{1,0:T(8,128)}) custom-call(f32[32,40,1280]{2,1,0:T(8,128)S(1)} %get-tuple-element.14.fine_in, f32[5,16,21,2,128]{4,3,2,1,0:T(2,128)S(1)} %get-tuple-element.15.medium_in, f32[2,160,160]{2,1,0:T(8,128)S(1)} %get-tuple-element.16.coarse_in, ...), custom_call_target="tpu_custom_call" | custom-call | tf_op jit(solution)/shard_map/pallas_call | solution.py:896

commit v4 on v3

--- a/solution.py
+++ b/solution.py
@@ -239,7 +239,7 @@
             return False
         if self.rows != self.n or self.members != self.lat or self.members != 16:
             return False
-        if self.fine % SUB or self.medium % 4 or self.fine != 2 * self.medium:
+        if self.fine_slots <= AHEAD * 2 * LANES or self.fine % SUB or self.medium % 4 or self.fine != 2 * self.medium:
             return False
         if self.fine_slots % (2 * LANES) or self.medium_slots % LANES or self.scale != 2:
             return False
@@ -273,6 +273,7 @@
     coarse_state,
     coarse_noise,
     coarse_basis,
+    begun,
     fine_next,
     medium_next,
     coarse_next,
@@ -308,6 +309,7 @@
     sent,
     came,
     twin,
+    here,
 ):
     n, lat = z.n, z.lat
     s, a = lax.axis_index("scale"), lax.axis_index("lat")
@@ -327,10 +329,15 @@
     owner = (a >= quarter) & (a < quarter + owners)
     mine = jnp.where(owner, a - quarter, 0)
 
+    step = jnp.where(a < lat // 2, -1, 1)
+
     def greet():
-        for i in range(1, lat):
-            near = {"scale": s, "lat": (a + i) % lat}
-            pl.semaphore_signal(barrier, inc=1, device_id=near, device_id_type=MESH)
+        @pl.when(owner)
+        def _():
+            for i in range(1, lat):
+                near = {"scale": s, "lat": (a + i) % lat}
+                pl.semaphore_signal(barrier, inc=1, device_id=near, device_id_type=MESH)
+
         pl.semaphore_signal(barrier, inc=1, device_id={"scale": 1 - s, "lat": a}, device_id_type=MESH)
 
     def coarse_loads():
@@ -488,17 +495,36 @@
         for r in range(z.rows):
             rows = rows_f[r * stride : r * stride + 2 * SUB, :]
             send[r] = (rows.astype(bf16).astype(f32) * scale_row).astype(bf16)
-        for i in range(1, lat):
-            row_copy(s * lat + (a + i) % lat).start()
-        pl.semaphore_wait(twin, 1)
-        for i in range(lat):
-            row_copy((1 - s) * lat + (a + i) % lat).start()
+        @pl.when(s == 1)
+        def _():
+            pl.semaphore_wait(twin, 1)
+            for p in range(2):
+                row_copy(p).start()
+
+        for p in range(lat):
+
+            @pl.when(a != p)
+            def _():
+                row_copy(s * lat + p).start()
+
+        @pl.when(s == 0)
+        def _():
+            pl.semaphore_wait(twin, 1)
+            for p in range(lat):
+                row_copy(lat + p).start()
+
+        @pl.when(s == 1)
+        def _():
+            for p in range(2, lat):
+                row_copy(p).start()
+
         got[me] = send[me]
 
     @jax.named_scope("send_first")
     def send_first():
+        turn = a
         for i in range(owners):
-            o = (a + i) % owners
+            o = (turn + i) % owners
 
             @pl.when(o + quarter != a)
             def _():
@@ -519,6 +545,19 @@
     def medium_chunk(t, _):
         for copy in medium_loads(t):
             copy.wait()
+        medium_work(t, 0)
+        return 0
+
+    @jax.named_scope("medium_pair")
+    def medium_pair(i, _):
+        for k in range(2):
+            for copy in medium_loads(1 + 2 * i + k):
+                copy.wait()
+        for k in range(2):
+            medium_work(1 + 2 * i + k, k)
+        return 0
+
+    def medium_work(t, slot):
         keep = room > t * LANES
         top = t * z.members * leap
         for e in range(z.members):
@@ -531,16 +570,15 @@
                 for c in range(2):
                     new = flat_next[pl.ds(top + 2 * (4 * q + b) + c, z.members, stride=leap), :]
                     at = q * LANES + b * z.pairs + c * z.members
-                    half_m[at : at + z.members, :] = new.astype(bf16)
+                    half_m[slot, at : at + z.members, :] = new.astype(bf16)
             basis = basis_m[t, 4 * q : 4 * q + 4].reshape(4 * z.rows, LANES)
             all_pairs = lax.dot_general(
-                basis, half_m[q * LANES : (q + 1) * LANES, :], (((1,), (1,)), ((), ())), preferred_element_type=f32
+                basis, half_m[slot, q * LANES : (q + 1) * LANES, :], (((1,), (1,)), ((), ())), preferred_element_type=f32
             )
             total = all_pairs[: z.rows]
             for b in range(1, 4):
                 total = jnp.where(lane4 == b, all_pairs[b * z.rows : (b + 1) * z.rows], total)
             picked_m[q * z.rows : (q + 1) * z.rows, :] += total
-        return 0
 
     @jax.named_scope("put_medium")
     def put_medium():
@@ -618,8 +656,12 @@
         for p in range(lat):
             rows = spread[p * pitch : p * pitch + SUB, :].astype(bf16).astype(f32)
             second[p] = (rows * scale_row).astype(bf16)
-        for i in range(1, lat):
-            second_copy((a + i) % lat).start()
+        for p in range(lat):
+
+            @pl.when(a != p)
+            def _():
+                second_copy(p).start()
+
         got_coarse[mine] = second[a]
 
     line_t = lax.broadcasted_iota(jnp.int32, (SUB, z.wrap), 0)
@@ -695,12 +737,40 @@
 
     @jax.named_scope("meet")
     def meet():
-        pl.semaphore_wait(barrier, lat)
+        @pl.when(owner)
+        def _():
+            pl.semaphore_wait(barrier, owners)
+
+        @pl.when(jnp.logical_not(owner))
+        def _():
+            pl.semaphore_wait(barrier, owners + 1)
+            for i in range(owners):
+                to = {"scale": s, "lat": quarter + (a + i) % owners}
+                pl.semaphore_signal(here, inc=1, device_id=to, device_id_type=MESH)
+
+    def tell_twin():
         pl.semaphore_signal(twin, inc=1, device_id={"scale": 1 - s, "lat": a}, device_id_type=MESH)
+
+    @jax.named_scope("hear")
+    def hear():
+        @pl.when(owner)
+        def _():
+            pl.semaphore_wait(here, lat - owners)
+            other = jnp.where(mine < quarter, mine, mine + owners)
+            pl.semaphore_signal(here, inc=1, device_id={"scale": s, "lat": other}, device_id_type=MESH)
+            tell_twin()
+
+    @jax.named_scope("meet_all")
+    def meet_all(who):
+        @pl.when(who)
+        def _():
+            pl.semaphore_wait(here, 1)
+            tell_twin()
 
     fine_count = (fine_limit + wide - 1) // wide
     half_way = jnp.minimum(fine_count, 3)
-    early = jnp.where(me < 2, half_way, jnp.where(me < SUB, 1, 0))
+    early = jnp.where(me < 2, 0, jnp.where(me < SUB - 2, 2, jnp.where(me < SUB, 1, 0)))
+    early = jnp.minimum(early, half_way)
     many = fine_count > 3
     start(coarse_loads())
     greet()
@@ -728,11 +798,19 @@
     meet()
     send_first()
     lax.fori_loop(early, half_way, fine_chunk, 0)
-    lax.fori_loop(0, (medium_limit + LANES - 1) // LANES, medium_chunk, 0)
+    medium_count = (medium_limit + LANES - 1) // LANES
+    some = jnp.minimum(medium_count, 1)
+    last = a >= quarter + owners
+    lax.fori_loop(0, some, medium_chunk, 0)
+    hear()
+    pairs = (medium_count - some) // 2
+    lax.fori_loop(0, pairs, medium_pair, 0)
+    lax.fori_loop(some + 2 * pairs, medium_count, medium_chunk, 0)
+    meet_all(last)
     lax.fori_loop(half_way, fine_count, fine_chunk, 0)
     put_fine(0, z.groups)
     put_medium()
-
+    meet_all(a < quarter)
     ship()
 
     @pl.when(owner)
@@ -746,11 +824,72 @@
     collect()
 
 
+AHEAD = 2
+
+
+def ahead_kernel(z, decay_in, amp_in, fine_state, fine_noise, out, state, noise, decay, amp, load, done):
+    me = lax.axis_index("scale") * z.lat + lax.axis_index("lat")
+    wide = 2 * LANES
+
+    def loads(k):
+        cols = pl.ds(k * wide, wide)
+        copies = [pltpu.make_async_copy(fine_state.at[:, :, cols], state.at[k], load.at[k])]
+        for g in range(z.groups):
+            rows = pl.ds(g * SUB, SUB)
+            copies.append(pltpu.make_async_copy(fine_noise.at[:, rows, cols], noise.at[k, g], load.at[k]))
+        return copies
+
+    def write(k):
+        return pltpu.make_async_copy(state.at[k], out.at[:, :, pl.ds(k * wide, wide)], done.at[k])
+
+    @pl.when(me < 2)
+    def _():
+        scalars = [pltpu.make_async_copy(decay_in, decay, done.at[0]), pltpu.make_async_copy(amp_in, amp, done.at[1])]
+        for copy in scalars:
+            copy.start()
+        for k in range(AHEAD):
+            for copy in loads(k):
+                copy.start()
+        for copy in scalars:
+            copy.wait()
+        slack = z.fine_slots - me * z.fine - lax.broadcasted_iota(jnp.int32, (SUB, wide), 0)
+        slack = slack - lax.broadcasted_iota(jnp.int32, (SUB, wide), 1)
+        for k in range(AHEAD):
+            for copy in loads(k):
+                copy.wait()
+
+            def pair(i, _):
+                two = pl.ds(2 * i, 2)
+                for g in range(z.groups):
+                    rows = slice(g * SUB, (g + 1) * SUB)
+                    keep = slack > g * SUB + k * wide
+                    new = decay[0] * state[k, two, rows, :] + amp[0] * noise[k, g, two].astype(jnp.float32)
+                    state[k, two, rows, :] = jnp.where(keep[None], new, 0.0)
+                return 0
+
+            lax.fori_loop(0, z.pairs // 2, pair, 0)
+            write(k).start()
+        for k in range(AHEAD):
+            write(k).wait()
+
+
 def grid_kernel(
-    z, fine_in, medium_in, coarse_in, got, got_coarse, table, fine_out, medium_out, coarse_out, out, turned, sems
+    z, fine_in, medium_in, coarse_in, got, got_coarse, table, begun, fine_out, medium_out, coarse_out, out, turned, sems
 ):
+    me = lax.axis_index("scale") * z.lat + lax.axis_index("lat")
+    wide = 2 * LANES
+
+    def ahead():
+        cols = pl.ds(0, AHEAD * wide)
+        return pltpu.make_async_copy(fine_in.at[:, :, cols], fine_out.at[:, :, cols], sems.at[2 + medium_in.shape[0]])
+
+    @pl.when(me >= 2)
+    def _():
+        ahead().start()
+
+    rest = pl.ds(AHEAD * wide, z.fine_slots - AHEAD * wide)
     copies = [
-        pltpu.make_async_copy(fine_in, fine_out, sems.at[0]),
+        pltpu.make_async_copy(fine_in.at[:, :, rest], fine_out.at[:, :, rest], sems.at[0]),
         pltpu.make_async_copy(coarse_in, coarse_out.at[0], sems.at[1]),
     ]
     for t in range(medium_in.shape[0]):
@@ -765,6 +904,10 @@
     with jax.named_scope("wait_writes"):
         for copy in copies:
             copy.wait()
+
+        @pl.when(me >= 2)
+        def _():
+            ahead().wait()
 
 
 def turn_rows(z, got, got_coarse, turned):
@@ -853,10 +996,26 @@
         pltpu.VMEM((owners, SUB, LANES), bf16),
         pltpu.VMEM((table_rows, 2 * z.wrap), bf16),
     )
+    begun = pl.pallas_call(
+        functools.partial(ahead_kernel, z),
+        out_shape=jax.ShapeDtypeStruct((z.pairs, z.fine, z.fine_slots), f32),
+        in_specs=[hbm] * 4,
+        out_specs=hbm,
+        scratch_shapes=[
+            pltpu.VMEM((AHEAD, z.pairs, z.fine, 2 * LANES), f32),
+            pltpu.VMEM((AHEAD, z.groups, z.pairs, SUB, 2 * LANES), bf16),
+            pltpu.SMEM((3,), f32),
+            pltpu.SMEM((3,), f32),
+            dma((AHEAD,)),
+            dma((AHEAD,)),
+        ],
+        compiler_params=pltpu.CompilerParams(vmem_limit_bytes=32 * 1024 * 1024),
+    )(*operands[:4])
+    begun = pltpu.with_memory_space_constraint(begun, pltpu.HBM)
     held = pl.pallas_call(
         functools.partial(spread_kernel, z),
         out_shape=between,
-        in_specs=[hbm] * 11,
+        in_specs=[hbm] * 12,
         out_specs=(vmem,) * 6,
         scratch_shapes=[
             pltpu.VMEM((z.groups, z.pairs, SUB, z.fine_slots), bf16),
@@ -865,7 +1024,7 @@
             pltpu.VMEM((z.groups * rows, 2 * LANES), f32),
             pltpu.VMEM((tiles, e, z.medium, 2, LANES), bf16),
             pltpu.VMEM((tiles, z.medium, rows, LANES), bf16),
-            pltpu.VMEM((z.medium * z.pairs, LANES), bf16),
+            pltpu.VMEM((2, z.medium * z.pairs, LANES), bf16),
             pltpu.VMEM((z.medium // 4 * rows, LANES), f32),
             pltpu.VMEM((rows * 3 * SUB, LANES), f32),
             pltpu.VMEM((n, 2 * SUB, LANES), bf16),
@@ -888,11 +1047,12 @@
             dma((3,)),
             dma((3,)),
             pltpu.SemaphoreType.REGULAR,
+            pltpu.SemaphoreType.REGULAR,
         ],
         compiler_params=pltpu.CompilerParams(
             collective_id=0, has_side_effects=True, vmem_limit_bytes=32 * 1024 * 1024
         ),
-    )(*operands)
+    )(*operands, begun)
     fine_next, medium_next, coarse_next, pattern = pl.pallas_call(
         functools.partial(grid_kernel, z),
         out_shape=(
@@ -901,11 +1061,12 @@
             jax.ShapeDtypeStruct(coarse_state.shape, f32),
             jax.ShapeDtypeStruct((e * NLON // LANES, LANES), f32),
         ),
-        in_specs=[vmem] * 6,
+        in_specs=[vmem] * 6 + [hbm],
         out_specs=(hbm, hbm, hbm, vmem),
-        scratch_shapes=[pltpu.VMEM((LANES, table_rows), bf16), dma((2 + tiles,))],
+        input_output_aliases={6: 0},
+        scratch_shapes=[pltpu.VMEM((LANES, table_rows), bf16), dma((3 + tiles,))],
         compiler_params=pltpu.CompilerParams(vmem_limit_bytes=32 * 1024 * 1024),
-    )(*held)
+    )(*held, begun)
     return (
         fine_next.reshape(fine_state.shape),
         medium_next.transpose(0, 2, 1, 3),

time: 20.2 us -> 19.3 us (0.955)
  Pallas kernels: 19.4 us -> 18.5 us
    pallas_call x1, Pallas kernels: 15.3 us -> 11.7 us  [fast_body(): pl.pallas_call(functools.partial(spread_kernel, z), out_shape=between, in...]
    pallas_call x0 -> x1, Pallas kernels: none -> 3.5 us  [fast_body(): pl.pallas_call(functools.partial(ahead_kernel, z), out_shape=jax.ShapeDty...]
    pallas_call x1, Pallas kernels: 4.1 us -> 3.27 us  [fast_body(): pl.pallas_call(functools.partial(grid_kernel, z), out_shape=(jax.ShapeDty...]
where the time goes in v4:
time: 19.3 us; the launch traced here: 19.1 us
  Pallas kernels  18.5 us (96%)
  between operations  0.65 us (3%)
    pallas_call x1, Pallas kernels, fast_body(): pl.pallas_call(functools.partial(spread_kernel, z), out_shape=between, in...  11.7 us
    pallas_call x1, Pallas kernels, fast_body(): pl.pallas_call(functools.partial(ahead_kernel, z), out_shape=jax.ShapeDty...  3.5 us
    pallas_call x1, Pallas kernels, fast_body(): pl.pallas_call(functools.partial(grid_kernel, z), out_shape=(jax.ShapeDty...  3.27 us

profile of v4, /device:TPU:0, one launch (start us, length us, event | category | flops | bytes accessed | tf_op | source)
XLA Modules:
  0.0 19.1 jit_solution(16723969683911632209)
XLA Ops:
  0.6 3.5 %shard_map.138.begun = f32[32,40,1280]{2,1,0:T(8,128)} custom-call(f32[3]{0:T(128)} %decay_in.3, f32[3]{0:T(128)} %amp_in.3, f32[32,40,1280]{2,1,0:T(8,128)} %bitcast.8, bf16[32,40,1280]{2,1,0:T(8,128)(2,1)} %bitcast.10), custom_call_target="tpu_custom_call" | custom-call | tf_op jit(solution)/shard_map/pallas_call | solution.py:999
  4.1 11.7 %shard_map.139 = (f32[32,40,1280]{2,1,0:T(8,128)S(1)}, f32[5,16,21,2,128]{4,3,2,1,0:T(2,128)S(1)}, f32[2,160,160]{2,1,0:T(8,128)S(1)}, bf16[32,16,128]{2,1,0:T(8...) custom-call(f32[3]{0:T(128)} %decay_in.3, f32[3]{0:T(128)} %amp_in.3, ...), custom_call_target="tpu_custom_call" | custom-call | tf_op jit(solution)/shard_map/pallas_call | solution.py:1015
  15.9 3.3 %shard_map.140 = (f32[32,40,1280]{2,1,0:T(8,128)}, f32[16,20,2,640]{3,2,1,0:T(2,128)}, f32[1,2,160,160]{3,2,1,0:T(8,128)}, f32[320,128]{1,0:T(8,128)}) custom-call(f32[32,40,1280]{2,1,0:T(8,128)S(1)} %get-tuple-element.14.fine_in, f32[5,16,21,2,128]{4,3,2,1,0:T(2,128)S(1)} %get-tuple-element.15.medium_in, ...), custom_call_target="tpu_custom_call", output_to_operand_aliasing={{0}: (6, {})} | custom-call | tf_op jit(solution)/shard_map/pallas_call | solution.py:1056
